TPU v7x, 512 devices: a whole 4x8x8 slice. The times are simulated.
512 devices in a mesh: row: 32 (over z, x_hi, core), col: 16 (over y, x_lo).
Axes of the slice: x: 4 (x_hi: 2, x_lo: 2; x = x_hi * 2 + x_lo), y: 8, z: 8, core: 2. Of those that a mesh axis runs over, the one named last changes fastest.
Arguments:
- reference_image: float32 [4096, 4096], P('row', 'col'), may hold values from -6 to 6
- source_images: float32 [4, 4096, 4096], P(None, 'row', 'col'), may hold values from -6 to 6
- hypotheses: int32 [8, 4096, 4096], P(None, 'row', 'col'), may hold values from 0 to 15
- source_ids: int32 [4], replicated, may hold values from 1 to 3
- coarse_disp: float32 [512, 512], P('col'), may hold values from 0 to 15
- coarse_conf: float32 [512, 512], P('col'), may hold values from 0.1 to 10
Outputs:
- disparity: float32 [4096, 4096], P('row', 'col')
All inputs are finite; a program needn't handle non-finite values.
Results may differ from a plain program's by a relative error of at most 0.0003.
Values sent between devices are 32-bit elements; how exact they have to be, the bound alone decides.
A program may use at most 64 MiB of HBM per device.

v0:
```python
import jax
import jax.numpy as jnp
from jax import lax
from jax.sharding import PartitionSpec as P

LEVELS = 16
HYP = 8
SRC = 4
WIN = 11
UPS = 8
CITER = 4
HALO = 50


smooth_pull = 1.0
previous_estimate_factor = 0.01
exponential_sharpness = 0.1
variance_floor = 1e-05


def extended_2(array, sides, width):
    for axis, dim in sides:
        size, length = (lax.axis_size(axis), array.shape[dim])
        up = [(i, (i + 1) % size) for i in range(size - 1)]
        down = [(j, i) for i, j in up]
        last = lax.slice_in_dim(array, length - width, length, axis=dim)
        initial = lax.slice_in_dim(array, 0, width, axis=dim)
        before = lax.ppermute(last, axis, up)
        after = lax.ppermute(initial, axis, down)
        array = jnp.concatenate([before, array, after], axis=dim)
    return array


def padded(array, sides, width):
    edges = {}
    for axis, dim in sides:
        size, length = (lax.axis_size(axis), array.shape[dim])
        up = [(i, (i + 1) % size) for i in range(size - 1)]
        last = lax.slice_in_dim(array, length - width, length, axis=dim)
        initial = lax.slice_in_dim(array, 0, width, axis=dim)
        edges[dim] = (
            lax.ppermute(last, axis, up),
            lax.ppermute(initial, axis, [(b, a) for a, b in up]),
        )
    done = []
    for _, dim in sides:
        low, high = edges[dim]
        around = [(width, width) if d in done else (0, 0) for d in range(array.ndim)]
        array = jnp.concatenate([jnp.pad(low, around), array, jnp.pad(high, around)], axis=dim)
        done.append(dim)
    return array


def interp_matrix(fine_start, fine_count, coarse_start, coarse_pixel_number, coarse_total):
    fine_pos = fine_start + jnp.arange(fine_count, dtype=jnp.int32)
    numerator = 2 * fine_pos + 1 - UPS
    lower = numerator // (2 * UPS)
    fraction = (numerator - lower * 2 * UPS).astype(jnp.float32) / (2.0 * UPS)
    low_index = jnp.clip(lower, 0, coarse_total - 1) - coarse_start
    high_index = jnp.clip(lower + 1, 0, coarse_total - 1) - coarse_start
    columns = jnp.arange(coarse_pixel_number, dtype=jnp.int32)
    low_part = jnp.where(columns[None, :] == low_index[:, None], 1.0 - fraction[:, None], 0.0)
    high_part = jnp.where(columns[None, :] == high_index[:, None], fraction[:, None], 0.0)
    return low_part + high_part


def jacobi_step(padded_line_span, disp, conf):
    middle = padded_line_span[1:-1]
    col_pad = jnp.pad(middle, ((0, 0), (1, 1)))
    neighbours = padded_line_span[:-2] + padded_line_span[2:] + col_pad[:, :-2] + col_pad[:, 2:]
    return (conf * disp + smooth_pull * neighbours) / (conf + 4.0 * smooth_pull)


def band_matrix(count):
    rows_pos = jnp.arange(count, dtype=jnp.int32)[:, None]
    cols_pos = jnp.arange(count + WIN - 1, dtype=jnp.int32)[None, :]
    offsets = cols_pos - rows_pos
    return jnp.where((offsets >= 0) & (offsets < WIN), 1.0, 0.0).astype(jnp.float32)


def window_box(maps, row_band, col_band):
    summed = jnp.einsum("ij,mjk->mik", row_band, maps, precision=lax.Precision.HIGHEST)
    return jnp.einsum("mik,lk->mil", summed, col_band, precision=lax.Precision.HIGHEST)


def estimate(chosen_hypothesis, candidate, centre):
    neighbour_jump_cost = (
        1.0 - chosen_hypothesis + previous_estimate_factor * (candidate - centre[None]) ** 2
    )
    candidate_mixing_shares = jnp.exp(-neighbour_jump_cost / exponential_sharpness)
    return jnp.sum(candidate_mixing_shares * candidate, axis=0) / jnp.sum(
        candidate_mixing_shares, axis=0
    )


def on_device(reference_image, source_images, hypotheses, source_ids, coarse_disp, coarse_conf):
    rows_tile, cols_tile = reference_image.shape
    row_count = lax.axis_size("row")
    col_count = lax.axis_size("col")
    row_index = lax.axis_index("row")
    col_index = lax.axis_index("col")
    radius = WIN // 2
    coarse_tile = rows_tile // UPS
    block_rows, coarse_cols = coarse_disp.shape
    coarse_height = block_rows * col_count
    whole_disp, whole_image_confidence = (
        lax.all_gather(coarse_disp, "col", axis=0, tiled=True),
        lax.all_gather(coarse_conf, "col", axis=0, tiled=True),
    )
    current = whole_disp
    for sweep in range(CITER):
        current = jacobi_step(
            jnp.pad(current, ((1, 1), (0, 0))), whole_disp, whole_image_confidence
        )
    padded_all = jnp.pad(current, ((1, 1), (0, 0)))
    coarse_piece = lax.dynamic_slice_in_dim(padded_all, row_index * coarse_tile, coarse_tile + 2, 0)
    row_mat = interp_matrix(
        row_index * rows_tile,
        rows_tile,
        row_index * coarse_tile - 1,
        coarse_tile + 2,
        coarse_height,
    )
    column_interp_weights = interp_matrix(
        col_index * cols_tile, cols_tile, 0, coarse_cols, coarse_cols
    )
    upsampled = jnp.dot(
        jnp.dot(row_mat, coarse_piece, precision=lax.Precision.HIGHEST),
        column_interp_weights.T,
        precision=lax.Precision.HIGHEST,
    )
    stacked = jnp.concatenate([reference_image[None], source_images], 0)
    padded_all = extended_2(stacked, (("row", 1), ("col", 2)), HALO)
    extended = padded_all[:, HALO - radius : HALO + rows_tile + radius, : HALO + cols_tile + radius]
    area = float(WIN * WIN)
    extended_width = extended.shape[2]
    row_band = band_matrix(rows_tile)
    wide_band = band_matrix(extended_width - 2 * radius)
    narrow_band = band_matrix(cols_tile)
    moments = (
        window_box(jnp.concatenate([extended, extended * extended], 0), row_band, wide_band) / area
    )
    channels = SRC + 1
    wide_mean = moments[:channels]
    wide_var = moments[channels:] - wide_mean**2 + variance_floor
    ref_begin = HALO - radius
    ref_mean = wide_mean[0][:, ref_begin : ref_begin + cols_tile]
    ref_var = wide_var[0][:, ref_begin : ref_begin + cols_tile]
    ref_window = extended[0][:, ref_begin : ref_begin + cols_tile + 2 * radius]

    def level_step(depth_level, chosen_hypothesis):
        begins = []
        elementwise_multiples = []
        for view_slot in range(SRC):
            begin_col = ref_begin - source_ids[view_slot] * depth_level
            begins.append(begin_col)
            src_window = lax.dynamic_slice_in_dim(
                extended[view_slot + 1], begin_col, cols_tile + 2 * radius, 1
            )
            elementwise_multiples.append(ref_window * src_window)
        cross_sums = window_box(jnp.stack(elementwise_multiples), row_band, narrow_band) / area
        ncc_sum = jnp.zeros((rows_tile, cols_tile), jnp.float32)
        for view_slot in range(SRC):
            mean_src = lax.dynamic_slice_in_dim(
                wide_mean[view_slot + 1], begins[view_slot], cols_tile, 1
            )
            var_src = lax.dynamic_slice_in_dim(
                wide_var[view_slot + 1], begins[view_slot], cols_tile, 1
            )
            ncc_sum = ncc_sum + (cross_sums[view_slot] - ref_mean * mean_src) / jnp.sqrt(
                ref_var * var_src
            )
        volume = ncc_sum / SRC
        return chosen_hypothesis + jnp.where(hypotheses == depth_level, volume[None], 0.0)

    chosen_hypothesis = lax.fori_loop(
        0, LEVELS, level_step, jnp.zeros((HYP, rows_tile, cols_tile), jnp.float32)
    )
    candidate = hypotheses.astype(jnp.float32)
    red = estimate(chosen_hypothesis, candidate, upsampled)
    red_ext = padded(red, (("row", 0), ("col", 1)), 1)
    neighbours = red_ext[:-2, 1:-1] + red_ext[2:, 1:-1] + red_ext[1:-1, :-2] + red_ext[1:-1, 2:]
    row_pos = row_index * rows_tile + jnp.arange(rows_tile, dtype=jnp.int32)
    col_pos = col_index * cols_tile + jnp.arange(cols_tile, dtype=jnp.int32)
    image_rows = rows_tile * row_count
    image_column_count = cols_tile * col_count
    vertical_strip_bounds = (row_pos == 0).astype(jnp.float32) + (row_pos == image_rows - 1).astype(
        jnp.float32
    )
    col_edges = (col_pos == 0).astype(jnp.float32) + (col_pos == image_column_count - 1).astype(
        jnp.float32
    )
    counted = 4.0 - vertical_strip_bounds[:, None] - col_edges[None, :]
    centre = 0.5 * upsampled + 0.5 * neighbours / counted
    black = estimate(chosen_hypothesis, candidate, centre)
    parity = (row_pos[:, None] + col_pos[None, :]) % 2 == 0
    return jnp.where(parity, red, black)


def solution(mesh):
    in_specs = (
        P("row", "col"),
        P(None, "row", "col"),
        P(None, "row", "col"),
        P(),
        P("col", None),
        P("col", None),
    )
    out_specs = P("row", "col")
    return jax.shard_map(
        on_device, mesh=mesh, in_specs=in_specs, out_specs=out_specs, check_vma=False
    )
```

profile of v0, /device:TPU:229, one launch (start us, length us, event | category | flops | bytes accessed | tf_op | source)
XLA Modules:
  0.0 318.0 jit_solution(13409691849801007548)
XLA Ops:
  8.4 2.6 collective-permute-start.1
  11.0 6.6 %collective-permute-start = (f32[5,50,256]{2,1,0:T(8,128)S(1)}, f32[5,50,256]{2,1,0:T(8,128)S(1)}, u32[]{:S(2)}, u32[]{:S(2)}) collective-permute-start(f32[5,50,256]{2,1,0:T(8,128)S(1)} %get-tuple-element.455), channel_id=1, source_target_pairs={{0,16},{16,32},{32,48},{48,64},{64,80},{80,96},{96,112},{112,128},... | collective-permute-start | bytes 768008 | tf_op jit(solution)/shard_map/ppermute | solution.py:28
  21.7 2.7 collective-permute-start.3
  24.7 2.6 collective-permute-start.2
  29.0 12.4 %collective-permute-done.3 = f32[5,228,50]{1,2,0:T(8,128)S(1)} collective-permute-done((f32[5,228,50]{1,2,0:T(8,128)S(1)}, f32[5,228,50]{1,2,0:T(8,128)S(1)}, u32[]{:S(2)}, u32[]{:S(2)}) %collective-permute-start.3) | collective-permute-done | bytes 228032 | tf_op jit(solution)/shard_map/ppermute | solution.py:29
  43.6 2.0 copy.21
  47.3 5.9 %fusion.55 = f32[10,311,128]{2,1,0:T(8,128)S(1)} fusion(f32[5,138,311]{2,1,0:T(8,128)S(1)} %get-tuple-element.425, f32[5,138,311]{2,1,0:T(8,128)S(1)} %get-tuple-element.574), kind=kOutput, calls=%fused_computation.70 | convolution fusion | flops 659737984 | bytes 3309040 | tf_op jit(solution)/shard_map/ij,mjk->mik/dot_general | solution.py:82
  53.2 2.7 fusion.61
  59.1 2.4 copy.26
  64.3 2.6 copy.24
  67.6 213.2 %while.17 = (s32[]{:T(128)}, f32[8,128,256]{2,1,0:T(8,128)S(1)}, s32[8,128,256]{2,1,0:T(8,128)S(1)}, f32[138,266]{1,0:T(8,128)}, f32[5,138,311]{2,1,0:T(8,128)S(...) while((s32[]{:T(128)}, f32[8,128,256]{2,1,0:T(8,128)S(1)}, ...), condition=%wide.region_1.2_spmd.clone, body=%wide.region_0.1_spmd.clone.sunk | while | flops 646766912 | bytes 25636720 | solution.py:176
  73.4 2.3 convolution_bitcast_fusion.2
  78.0 1.6 fusion.173
  86.7 2.3 convolution_bitcast_fusion.2
  91.4 1.6 fusion.173
  100.0 2.3 convolution_bitcast_fusion.2
  104.7 1.7 fusion.173
  113.3 2.3 convolution_bitcast_fusion.2
  118.0 1.6 fusion.173
  126.7 2.3 convolution_bitcast_fusion.2
  131.3 1.6 fusion.173
  140.0 2.3 convolution_bitcast_fusion.2
  144.7 1.6 fusion.173
  153.3 2.3 convolution_bitcast_fusion.2
  158.0 1.6 fusion.173
  166.6 2.3 convolution_bitcast_fusion.2
  171.3 1.6 fusion.173
  180.0 2.3 convolution_bitcast_fusion.2
  184.6 1.6 fusion.173
  193.3 2.3 convolution_bitcast_fusion.2
  198.0 1.6 fusion.173
  206.6 2.3 convolution_bitcast_fusion.2
  211.3 1.6 fusion.173
  219.9 2.3 convolution_bitcast_fusion.2
  224.6 1.6 fusion.173
  233.2 2.3 convolution_bitcast_fusion.2
  237.9 1.6 fusion.173
  246.6 2.3 convolution_bitcast_fusion.2
  251.2 1.6 fusion.173
  259.9 2.3 convolution_bitcast_fusion.2
  264.6 1.6 fusion.173
  273.2 2.3 convolution_bitcast_fusion.2
  280.8 4.1 %fusion.67 = (f32[512,512]{1,0:T(8,128)S(1)}, f32[512,512]{1,0:T(8,128)S(1)}) fusion(f32[512,512]{1,0:T(8,128)} %all-gather.5.cloned.1.call-done, f32[512,512]{1,0:T(8,128)} %all-gather.3.cloned.1.call-done), kind=kLoop, calls=%fused_computation.95 | loop fusion | flops 1835008 | bytes 4194304 | tf_op jit(solution)/shard_map/div | solution.py:71
  289.0 4.4 %collective-permute-start.7 = (f32[128,1]{1,0:T(8,128)S(1)}, f32[128,1]{1,0:T(8,128)S(1)}, u32[]{:S(2)}, u32[]{:S(2)}) collective-permute-start(f32[128,1]{1,0:T(8,128)S(1)} %get-tuple-element.458), channel_id=1, source_target_pairs={{1,0},{2,1},{3,2},{4,3},{5,4},{6,5},{7,6},{8,7},{9,8},{10,9},{11,1... | collective-permute-start | bytes 1544 | tf_op jit(solution)/shard_map/ppermute | solution.py:43
  293.5 2.7 collective-permute-start.5
  296.2 6.4 %collective-permute-start.4 = (f32[1,256]{1,0:T(1,128)S(1)}, f32[1,256]{1,0:T(1,128)S(1)}, u32[]{:S(2)}, u32[]{:S(2)}) collective-permute-start(f32[1,256]{1,0:T(1,128)S(1)} %get-tuple-element.459), channel_id=1, source_target_pairs={{0,16},{16,32},{32,48},{48,64},{64,80},{80,96},{96,112},{112,128},... | collective-permute-start | bytes 3080 | tf_op jit(solution)/shard_map/ppermute | solution.py:42
  302.6 2.0 collective-permute-start.6
  304.7 5.1 %collective-permute-done.6 = f32[128,1]{1,0:T(8,128)S(1)} collective-permute-done((f32[128,1]{1,0:T(8,128)S(1)}, f32[128,1]{1,0:T(8,128)S(1)}, u32[]{:S(2)}, u32[]{:S(2)}) %collective-permute-start.6) | collective-permute-done | bytes 544 | tf_op jit(solution)/shard_map/ppermute | solution.py:42
  (308 shorter events, 133.9 us)
Async XLA Ops:
  6.5 14.6 %copy-start.6 = (f32[4,128,256]{2,1,0:T(8,128)S(1)}, f32[4,128,256]{2,1,0:T(8,128)}, u32[]{:S(2)}) copy-start(f32[4,128,256]{2,1,0:T(8,128)} %param.9) | copy-start | bytes 1572868
  6.5 14.6 %copy-start.8 = (f32[128,256]{1,0:T(8,128)S(1)}, f32[128,256]{1,0:T(8,128)}, u32[]{:S(2)}) copy-start(f32[128,256]{1,0:T(8,128)} %param.8) | copy-start | bytes 393220
  6.5 274.3 %all-gather.5.cloned.1.call-start = ((), (), s32[]{:S(2)}) async-start(), calls=%async_computation.1 | async-start | bytes 1114112 | tf_op jit(solution)/shard_map/all_gather | solution.py:107
  7.3 273.5 %all-gather.3.cloned.1.call-start = ((), (), s32[]{:S(2)}) async-start(), calls=%async_computation | async-start | bytes 1114112 | tf_op jit(solution)/shard_map/all_gather | solution.py:108
  8.4 11.7 %collective-permute-start.1 = (f32[5,50,256]{2,1,0:T(8,128)S(1)}, f32[5,50,256]{2,1,0:T(8,128)S(1)}, u32[]{:S(2)}, u32[]{:S(2)}) collective-permute-start(f32[5,50,256]{2,1,0:T(8,128)S(1)} %get-tuple-element.456), channel_id=1, source_target_pairs={{16,0},{32,16},{48,32},{64,48},{80,64},{96,80},{112,96},{128,112},... | collective-permute-start | bytes 768008 | tf_op jit(solution)/shard_map/ppermute | solution.py:29
  11.0 10.2 %collective-permute-start = (f32[5,50,256]{2,1,0:T(8,128)S(1)}, f32[5,50,256]{2,1,0:T(8,128)S(1)}, u32[]{:S(2)}, u32[]{:S(2)}) collective-permute-start(f32[5,50,256]{2,1,0:T(8,128)S(1)} %get-tuple-element.455), channel_id=1, source_target_pairs={{0,16},{16,32},{32,48},{48,64},{64,80},{80,96},{96,112},{112,128},... | collective-permute-start | bytes 768008 | tf_op jit(solution)/shard_map/ppermute | solution.py:28
  21.7 19.7 %collective-permute-start.3 = (f32[5,228,50]{1,2,0:T(8,128)S(1)}, f32[5,228,50]{1,2,0:T(8,128)S(1)}, u32[]{:S(2)}, u32[]{:S(2)}) collective-permute-start(f32[5,228,50]{1,2,0:T(8,128)S(1)} %copy.20), channel_id=1, source_target_pairs={{1,0},{2,1},{3,2},{4,3},{5,4},{6,5},{7,6},{8,7},{9,8},{10,9},{11,1... | collective-permute-start | bytes 684008 | tf_op jit(solution)/shard_map/ppermute | solution.py:29
  24.5 21.2 %copy-start.9 = (f32[128,256]{1,0:T(8,128)S(1)}, f32[128,256]{1,0:T(8,128)}, u32[]{:S(2)}) copy-start(f32[128,256]{1,0:T(8,128)} %param.8) | copy-start | bytes 393220
  24.7 18.9 %collective-permute-start.2 = (f32[5,228,50]{1,2,0:T(8,128)S(1)}, f32[5,228,50]{1,2,0:T(8,128)}, u32[]{:S(2)}, u32[]{:S(2)}) collective-permute-start(f32[5,228,50]{1,2,0:T(8,128)S(1)} %copy.19), channel_id=1, source_target_pairs={{0,1},{1,2},{2,3},{3,4},{4,5},{5,6},{6,7},{7,8},{8,9},{9,10},{10,1... | collective-permute-start | bytes 684008 | tf_op jit(solution)/shard_map/ppermute | solution.py:28
  67.6 5.7 %copy-start.1 = (f32[5,138,311]{2,1,0:T(8,128)}, f32[5,138,311]{2,1,0:T(8,128)S(1)}, u32[]{:S(2)}) copy-start(f32[5,138,311]{2,1,0:T(8,128)S(1)} %get-tuple-element.604) | copy-start | bytes 2575084 | tf_op jit(solution)/shard_map/while
  73.3 3.7 %copy-start.3 = (f32[5,128,301]{2,1,0:T(8,128)S(1)}, f32[5,128,301]{2,1,0:T(8,128)}, u32[]{:S(2)}) copy-start(f32[5,128,301]{2,1,0:T(8,128)} %get-tuple-element.609) | copy-start | bytes 2311684 | tf_op jit(solution)/shard_map/while
  73.4 3.7 %copy-start.4 = (f32[5,128,301]{2,1,0:T(8,128)S(1)}, f32[5,128,301]{2,1,0:T(8,128)}, u32[]{:S(2)}) copy-start(f32[5,128,301]{2,1,0:T(8,128)} %get-tuple-element.607) | copy-start | bytes 2311684 | tf_op jit(solution)/shard_map/while
  80.9 5.7 %copy-start.1 = (f32[5,138,311]{2,1,0:T(8,128)}, f32[5,138,311]{2,1,0:T(8,128)S(1)}, u32[]{:S(2)}) copy-start(f32[5,138,311]{2,1,0:T(8,128)S(1)} %get-tuple-element.604) | copy-start | bytes 2575084 | tf_op jit(solution)/shard_map/while
  86.7 3.7 %copy-start.3 = (f32[5,128,301]{2,1,0:T(8,128)S(1)}, f32[5,128,301]{2,1,0:T(8,128)}, u32[]{:S(2)}) copy-start(f32[5,128,301]{2,1,0:T(8,128)} %get-tuple-element.609) | copy-start | bytes 2311684 | tf_op jit(solution)/shard_map/while
  86.7 3.7 %copy-start.4 = (f32[5,128,301]{2,1,0:T(8,128)S(1)}, f32[5,128,301]{2,1,0:T(8,128)}, u32[]{:S(2)}) copy-start(f32[5,128,301]{2,1,0:T(8,128)} %get-tuple-element.607) | copy-start | bytes 2311684 | tf_op jit(solution)/shard_map/while
  94.3 5.7 %copy-start.1 = (f32[5,138,311]{2,1,0:T(8,128)}, f32[5,138,311]{2,1,0:T(8,128)S(1)}, u32[]{:S(2)}) copy-start(f32[5,138,311]{2,1,0:T(8,128)S(1)} %get-tuple-element.604) | copy-start | bytes 2575084 | tf_op jit(solution)/shard_map/while
  100.0 3.7 %copy-start.3 = (f32[5,128,301]{2,1,0:T(8,128)S(1)}, f32[5,128,301]{2,1,0:T(8,128)}, u32[]{:S(2)}) copy-start(f32[5,128,301]{2,1,0:T(8,128)} %get-tuple-element.609) | copy-start | bytes 2311684 | tf_op jit(solution)/shard_map/while
  100.0 3.7 %copy-start.4 = (f32[5,128,301]{2,1,0:T(8,128)S(1)}, f32[5,128,301]{2,1,0:T(8,128)}, u32[]{:S(2)}) copy-start(f32[5,128,301]{2,1,0:T(8,128)} %get-tuple-element.607) | copy-start | bytes 2311684 | tf_op jit(solution)/shard_map/while
  107.6 5.7 %copy-start.1 = (f32[5,138,311]{2,1,0:T(8,128)}, f32[5,138,311]{2,1,0:T(8,128)S(1)}, u32[]{:S(2)}) copy-start(f32[5,138,311]{2,1,0:T(8,128)S(1)} %get-tuple-element.604) | copy-start | bytes 2575084 | tf_op jit(solution)/shard_map/while
  120.9 5.7 %copy-start.1 = (f32[5,138,311]{2,1,0:T(8,128)}, f32[5,138,311]{2,1,0:T(8,128)S(1)}, u32[]{:S(2)}) copy-start(f32[5,138,311]{2,1,0:T(8,128)S(1)} %get-tuple-element.604) | copy-start | bytes 2575084 | tf_op jit(solution)/shard_map/while
  126.6 3.7 %copy-start.3 = (f32[5,128,301]{2,1,0:T(8,128)S(1)}, f32[5,128,301]{2,1,0:T(8,128)}, u32[]{:S(2)}) copy-start(f32[5,128,301]{2,1,0:T(8,128)} %get-tuple-element.609) | copy-start | bytes 2311684 | tf_op jit(solution)/shard_map/while
  126.7 3.7 %copy-start.4 = (f32[5,128,301]{2,1,0:T(8,128)S(1)}, f32[5,128,301]{2,1,0:T(8,128)}, u32[]{:S(2)}) copy-start(f32[5,128,301]{2,1,0:T(8,128)} %get-tuple-element.607) | copy-start | bytes 2311684 | tf_op jit(solution)/shard_map/while
  134.2 5.7 %copy-start.1 = (f32[5,138,311]{2,1,0:T(8,128)}, f32[5,138,311]{2,1,0:T(8,128)S(1)}, u32[]{:S(2)}) copy-start(f32[5,138,311]{2,1,0:T(8,128)S(1)} %get-tuple-element.604) | copy-start | bytes 2575084 | tf_op jit(solution)/shard_map/while
  140.0 3.7 %copy-start.3 = (f32[5,128,301]{2,1,0:T(8,128)S(1)}, f32[5,128,301]{2,1,0:T(8,128)}, u32[]{:S(2)}) copy-start(f32[5,128,301]{2,1,0:T(8,128)} %get-tuple-element.609) | copy-start | bytes 2311684 | tf_op jit(solution)/shard_map/while
  140.0 3.7 %copy-start.4 = (f32[5,128,301]{2,1,0:T(8,128)S(1)}, f32[5,128,301]{2,1,0:T(8,128)}, u32[]{:S(2)}) copy-start(f32[5,128,301]{2,1,0:T(8,128)} %get-tuple-element.607) | copy-start | bytes 2311684 | tf_op jit(solution)/shard_map/while
  147.6 5.7 %copy-start.1 = (f32[5,138,311]{2,1,0:T(8,128)}, f32[5,138,311]{2,1,0:T(8,128)S(1)}, u32[]{:S(2)}) copy-start(f32[5,138,311]{2,1,0:T(8,128)S(1)} %get-tuple-element.604) | copy-start | bytes 2575084 | tf_op jit(solution)/shard_map/while
  153.3 3.7 %copy-start.3 = (f32[5,128,301]{2,1,0:T(8,128)S(1)}, f32[5,128,301]{2,1,0:T(8,128)}, u32[]{:S(2)}) copy-start(f32[5,128,301]{2,1,0:T(8,128)} %get-tuple-element.609) | copy-start | bytes 2311684 | tf_op jit(solution)/shard_map/while
  153.3 3.7 %copy-start.4 = (f32[5,128,301]{2,1,0:T(8,128)S(1)}, f32[5,128,301]{2,1,0:T(8,128)}, u32[]{:S(2)}) copy-start(f32[5,128,301]{2,1,0:T(8,128)} %get-tuple-element.607) | copy-start | bytes 2311684 | tf_op jit(solution)/shard_map/while
  160.9 5.7 %copy-start.1 = (f32[5,138,311]{2,1,0:T(8,128)}, f32[5,138,311]{2,1,0:T(8,128)S(1)}, u32[]{:S(2)}) copy-start(f32[5,138,311]{2,1,0:T(8,128)S(1)} %get-tuple-element.604) | copy-start | bytes 2575084 | tf_op jit(solution)/shard_map/while
  166.6 3.7 %copy-start.3 = (f32[5,128,301]{2,1,0:T(8,128)S(1)}, f32[5,128,301]{2,1,0:T(8,128)}, u32[]{:S(2)}) copy-start(f32[5,128,301]{2,1,0:T(8,128)} %get-tuple-element.609) | copy-start | bytes 2311684 | tf_op jit(solution)/shard_map/while
  166.6 3.7 %copy-start.4 = (f32[5,128,301]{2,1,0:T(8,128)S(1)}, f32[5,128,301]{2,1,0:T(8,128)}, u32[]{:S(2)}) copy-start(f32[5,128,301]{2,1,0:T(8,128)} %get-tuple-element.607) | copy-start | bytes 2311684 | tf_op jit(solution)/shard_map/while
  174.2 5.7 %copy-start.1 = (f32[5,138,311]{2,1,0:T(8,128)}, f32[5,138,311]{2,1,0:T(8,128)S(1)}, u32[]{:S(2)}) copy-start(f32[5,138,311]{2,1,0:T(8,128)S(1)} %get-tuple-element.604) | copy-start | bytes 2575084 | tf_op jit(solution)/shard_map/while
  179.9 3.7 %copy-start.3 = (f32[5,128,301]{2,1,0:T(8,128)S(1)}, f32[5,128,301]{2,1,0:T(8,128)}, u32[]{:S(2)}) copy-start(f32[5,128,301]{2,1,0:T(8,128)} %get-tuple-element.609) | copy-start | bytes 2311684 | tf_op jit(solution)/shard_map/while
  179.9 3.7 %copy-start.4 = (f32[5,128,301]{2,1,0:T(8,128)S(1)}, f32[5,128,301]{2,1,0:T(8,128)}, u32[]{:S(2)}) copy-start(f32[5,128,301]{2,1,0:T(8,128)} %get-tuple-element.607) | copy-start | bytes 2311684 | tf_op jit(solution)/shard_map/while
  187.5 5.7 %copy-start.1 = (f32[5,138,311]{2,1,0:T(8,128)}, f32[5,138,311]{2,1,0:T(8,128)S(1)}, u32[]{:S(2)}) copy-start(f32[5,138,311]{2,1,0:T(8,128)S(1)} %get-tuple-element.604) | copy-start | bytes 2575084 | tf_op jit(solution)/shard_map/while
  200.9 5.7 %copy-start.1 = (f32[5,138,311]{2,1,0:T(8,128)}, f32[5,138,311]{2,1,0:T(8,128)S(1)}, u32[]{:S(2)}) copy-start(f32[5,138,311]{2,1,0:T(8,128)S(1)} %get-tuple-element.604) | copy-start | bytes 2575084 | tf_op jit(solution)/shard_map/while
  214.2 5.7 %copy-start.1 = (f32[5,138,311]{2,1,0:T(8,128)}, f32[5,138,311]{2,1,0:T(8,128)S(1)}, u32[]{:S(2)}) copy-start(f32[5,138,311]{2,1,0:T(8,128)S(1)} %get-tuple-element.604) | copy-start | bytes 2575084 | tf_op jit(solution)/shard_map/while
  227.5 5.7 %copy-start.1 = (f32[5,138,311]{2,1,0:T(8,128)}, f32[5,138,311]{2,1,0:T(8,128)S(1)}, u32[]{:S(2)}) copy-start(f32[5,138,311]{2,1,0:T(8,128)S(1)} %get-tuple-element.604) | copy-start | bytes 2575084 | tf_op jit(solution)/shard_map/while
  240.8 5.7 %copy-start.1 = (f32[5,138,311]{2,1,0:T(8,128)}, f32[5,138,311]{2,1,0:T(8,128)S(1)}, u32[]{:S(2)}) copy-start(f32[5,138,311]{2,1,0:T(8,128)S(1)} %get-tuple-element.604) | copy-start | bytes 2575084 | tf_op jit(solution)/shard_map/while
  254.1 5.7 %copy-start.1 = (f32[5,138,311]{2,1,0:T(8,128)}, f32[5,138,311]{2,1,0:T(8,128)S(1)}, u32[]{:S(2)}) copy-start(f32[5,138,311]{2,1,0:T(8,128)S(1)} %get-tuple-element.604) | copy-start | bytes 2575084 | tf_op jit(solution)/shard_map/while
  267.5 5.7 %copy-start.1 = (f32[5,138,311]{2,1,0:T(8,128)}, f32[5,138,311]{2,1,0:T(8,128)S(1)}, u32[]{:S(2)}) copy-start(f32[5,138,311]{2,1,0:T(8,128)S(1)} %get-tuple-element.604) | copy-start | bytes 2575084 | tf_op jit(solution)/shard_map/while
  280.8 4.1 %copy-start.5 = (f32[512,512]{1,0:T(8,128)S(1)}, f32[512,512]{1,0:T(8,128)}, u32[]{:S(2)}) copy-start(f32[512,512]{1,0:T(8,128)} %all-gather.3.cloned.1.call-done) | copy-start | bytes 3145732
  288.5 21.3 %copy-start.13 = (f32[256]{0:T(256)S(1)}, f32[256]{0:T(256)}, u32[]{:S(2)}) copy-start(f32[256]{0:T(256)} %fusion.133) | copy-start | bytes 3076
  288.5 21.3 %copy-start.18 = (f32[128]{0:T(128)S(1)}, f32[128]{0:T(128)}, u32[]{:S(2)}) copy-start(f32[128]{0:T(128)} %fusion.135) | copy-start | bytes 1540
  289.0 15.6 %collective-permute-start.7 = (f32[128,1]{1,0:T(8,128)S(1)}, f32[128,1]{1,0:T(8,128)S(1)}, u32[]{:S(2)}, u32[]{:S(2)}) collective-permute-start(f32[128,1]{1,0:T(8,128)S(1)} %get-tuple-element.458), channel_id=1, source_target_pairs={{1,0},{2,1},{3,2},{4,3},{5,4},{6,5},{7,6},{8,7},{9,8},{10,9},{11,1... | collective-permute-start | bytes 1544 | tf_op jit(solution)/shard_map/ppermute | solution.py:43
  293.5 16.3 %collective-permute-start.5 = (f32[1,256]{1,0:T(1,128)S(1)}, f32[1,256]{1,0:T(1,128)S(1)}, u32[]{:S(2)}, u32[]{:S(2)}) collective-permute-start(f32[1,256]{1,0:T(1,128)S(1)} %get-tuple-element.460), channel_id=1, source_target_pairs={{16,0},{32,16},{48,32},{64,48},{80,64},{96,80},{112,96},{128,112},... | collective-permute-start | bytes 3080 | tf_op jit(solution)/shard_map/ppermute | solution.py:43
  296.2 13.6 %collective-permute-start.4 = (f32[1,256]{1,0:T(1,128)S(1)}, f32[1,256]{1,0:T(1,128)S(1)}, u32[]{:S(2)}, u32[]{:S(2)}) collective-permute-start(f32[1,256]{1,0:T(1,128)S(1)} %get-tuple-element.459), channel_id=1, source_target_pairs={{0,16},{16,32},{32,48},{48,64},{64,80},{80,96},{96,112},{112,128},... | collective-permute-start | bytes 3080 | tf_op jit(solution)/shard_map/ppermute | solution.py:42
  302.6 7.1 %collective-permute-start.6 = (f32[128,1]{1,0:T(8,128)S(1)}, f32[128,1]{1,0:T(8,128)S(1)}, u32[]{:S(2)}, u32[]{:S(2)}) collective-permute-start(f32[128,1]{1,0:T(8,128)S(1)} %get-tuple-element.457), channel_id=1, source_target_pairs={{0,1},{1,2},{2,3},{3,4},{4,5},{5,6},{6,7},{7,8},{8,9},{9,10},{10,1... | collective-permute-start | bytes 1544 | tf_op jit(solution)/shard_map/ppermute | solution.py:42
  (43 other events, 96.5 us)
Sparse Core Ops, SparseCore 0:
  9.4 69.4 all-gather.4
  81.0 68.8 all-gather.2
where the time goes:
time: 320 us; the launch traced here: 318 us
  other arithmetic  75 us (23%)
  matrix products  68.9 us (22%)
  local copies, waits for them, and re-layouts  66.7 us (21%)
  loops' own time  42 us (13%)
  starting transfers between devices  30.1 us (9%)
  waiting for transfers between devices  21.7 us (7%)
  between operations  13.7 us (4%)
    dot_general x17, matrix products, window_box(): jnp.einsum('ij,mjk->mik', row_band, maps, precision=lax.Precision.HIGHEST)  42.3 us
    another operation x1, loops' own time, on_device(): lax.fori_loop(0, LEVELS, level_step, jnp.zeros((HYP, rows_tile, cols_tile...  42 us
    broadcast_in_dim x16, other arithmetic, level_step(): jnp.where(hypotheses == depth_level, volume[None], 0.0)  26.4 us
    dot_general x17, matrix products, window_box(): jnp.einsum('mik,lk->mil', summed, col_band, precision=lax.Precision.HIGHEST)  25.4 us
    mul x16, other arithmetic, level_step(): elementwise_multiples.append(ref_window * src_window)  25.3 us
    slice x16, local copies, waits for them, and re-layouts, level_step(): wide_mean[view_slot + 1]  15.3 us
    slice x16, local copies, waits for them, and re-layouts, level_step(): extended[view_slot + 1]  14.4 us
    ppermute x2, waiting for transfers between devices, extended_2(): after = lax.ppermute(initial, axis, down)  13.7 us
  transfers between devices with their start and end apart: 10, of which 5 were waited for; matrix products, arithmetic and copies ran while one was open for 59% of the time, Pallas kernels for 0%

commit v1 on v0

v1 whole, which is shorter than its diff:
```python
import functools

import jax
import jax.numpy as jnp
from jax import lax
from jax.experimental import pallas as pl
from jax.experimental.pallas import tpu as pltpu
from jax.sharding import PartitionSpec as P

LEVELS = 16
HYP = 8
SRC = 4
MAXID = 3
WIN = 11
UPS = 8
CITER = 4
R = WIN // 2
AREA = float(WIN * WIN)
FLOOR = 1e-05

ROWS, COLS = 128, 256
SEGS = 8
SEG = COLS // SEGS
SHIFT = MAXID * (LEVELS - 1)
LEFT = SHIFT + R
PADL = 56
CI = 320
NJ = SEG + 2 * R + SHIFT
NK = SEG + 2 * R
NM = SEG + SHIFT
HL = 2 * R
bf16 = jnp.bfloat16
f32 = jnp.float32


def window11(vals):
    n = len(vals)
    count = n - WIN + 1
    suf, pre = {}, {}
    for start in range(0, n, WIN):
        stop = min(start + WIN, n)
        if stop - start == WIN and start < count:
            acc = vals[stop - 1]
            suf[stop - 1] = acc
            for i in range(stop - 2, start - 1, -1):
                acc = vals[i] + acc
                suf[i] = acc
        if start:
            acc = vals[start]
            pre[start] = acc
            for i in range(start + 1, min(stop, start + WIN - 1)):
                acc = acc + vals[i]
                pre[i] = acc
    return [suf[i] if i % WIN == 0 else suf[i] + pre[i + WIN - 1] for i in range(count)]


def parts(value, count):
    out = []
    for _ in range(count - 1):
        piece = value.astype(bf16)
        out.append(piece)
        value = value - piece.astype(f32)
    out.append(value.astype(bf16))
    return out


def put_parts(ref, sums, columns):
    n = len(sums)
    for q in range(0, n, 2):
        both = jnp.concatenate(sums[q:q + 2], axis=0) if q + 1 < n else sums[q]
        for piece, col in zip(parts(both, len(columns)), columns):
            ref[8 * q:8 * q + both.shape[0], col:col + 128] = piece


def band_main():
    a = lax.broadcasted_iota(jnp.int32, (ROWS, ROWS), 0)
    b = lax.broadcasted_iota(jnp.int32, (ROWS, ROWS), 1)
    return jnp.where(jnp.abs(a - b) <= R, 1.0, 0.0).astype(bf16)


def band_halo(view):
    a = lax.broadcasted_iota(jnp.int32, (128, ROWS), 0) - view * HL
    b = lax.broadcasted_iota(jnp.int32, (128, ROWS), 1)
    row = jnp.where(a < R, a - R, a - R + ROWS)
    good = (a >= 0) & (a < HL) & (jnp.abs(row - b) <= R)
    return jnp.where(good, 1.0, 0.0).astype(bf16)


def score_kernel(ids, xm, xh, hyp, up, sel_out, ht_out, red_out,
                 xs, hs, rt, rx3, rmom, xmom, lmom, cmom, av, bv, lhs, lx, yy, vol, htc):
    zero = jnp.zeros((128, 128), bf16)
    b = band_main()
    halo = [band_halo(v) for v in range(SRC)]
    rt[0:128, 0:128] = b
    rt[0:128, 128:256] = zero
    rt[128:256, 0:128] = zero
    rt[128:256, 128:256] = b
    for v in range(SRC):
        rmom[v, 0:128, 0:128] = halo[v]
        rmom[v, 0:128, 128:256] = zero
        rmom[v, 128:256, 0:128] = zero
        rmom[v, 128:256, 128:256] = halo[v]
        p, q = v // 2, v % 2
        rx3[p, 0:128, 128 * q:128 * q + 128] = halo[v]
        rx3[p, 128:256, 128 * q:128 * q + 128] = halo[v]

    for j in range(NJ):
        rows = pl.ds(j + PADL - LEFT, SEGS, stride=SEG)
        for v in range(SRC):
            xs[v + 1, j] = xm[v + 1, rows, :]
        hs[1, j] = xh[1, rows, :]
        if j >= SHIFT:
            xs[0, j] = xm[0, rows, :]
            hs[0, j] = xh[0, rows, :]

    packed = hyp[0]
    for k in range(1, HYP):
        packed = packed | (hyp[k] << (4 * k))
    htc[...] = packed.T
    for i in range(SEG):
        ht_out[8 * i:8 * i + 8, :] = htc[pl.ds(i, SEGS, stride=SEG), :]

    def moments(load, first, count, ref):
        vals = [load(first + j) for j in range(count)]
        put_parts(ref, window11(vals), (0, 256, 512))
        vals = [load(first + j) for j in range(count)]
        put_parts(ref, window11([x * x for x in vals]), (128, 384, 640))

    def finish(rows, view):
        total = jnp.dot(lmom[0:rows, 0:256], rt[...], preferred_element_type=f32)
        for t in (256, 512):
            total += jnp.dot(lmom[0:rows, t:t + 256], rt[...], preferred_element_type=f32)
        for t in (0, 256, 512):
            total += jnp.dot(xmom[0:rows, t:t + 256], rmom[view], preferred_element_type=f32)
        cmom[0:rows, :] = total

    moments(lambda j: hs[0, j], SHIFT, NK, xmom)
    moments(lambda j: xs[0, j], SHIFT, NK, lmom)
    finish(SEG * 8, 0)
    for i in range(SEG):
        m = cmom[8 * i:8 * i + 8, 0:128] / AREA
        var = cmom[8 * i:8 * i + 8, 128:256] / AREA - m * m + FLOOR
        av[0, i] = lax.rsqrt(var)
        bv[0, i] = m

    moments(lambda j: hs[1, j], 0, NJ, xmom)

    def view_moments(v, carry):
        moments(lambda j: xs[v + 1, j], 0, NJ, lmom)
        finish(NM * 8, v)

        def fill(i, c):
            rows = pl.ds(pl.multiple_of(8 * i, 8), 8)
            m = cmom[rows, 0:128] / AREA
            var = cmom[rows, 128:256] / AREA - m * m + FLOOR
            inv = lax.rsqrt(var) / SRC
            av[v + 1, i] = inv / AREA
            bv[v + 1, i] = m * inv
            return c

        return lax.fori_loop(0, NM, fill, carry)

    lax.fori_loop(0, SRC, view_moments, 0)

    lane = lax.broadcasted_iota(jnp.int32, (8, 128), 1)
    masks = [lane < HL * (v + 1) for v in range(SRC - 1)]

    def level(l, carry):
        begins = [SHIFT - ids[v] * l for v in range(SRC)]
        prods = []
        for k in range(NK):
            piece = hs[1, begins[3] + k]
            for v in (2, 1, 0):
                piece = jnp.where(masks[v], hs[1, begins[v] + k], piece)
            prods.append(hs[0, SHIFT + k] * piece)
        put_parts(lx, window11(prods), (0, 128))
        for v in range(SRC):
            prods = [xs[0, SHIFT + k] * xs[v + 1, begins[v] + k] for k in range(NK)]
            put_parts(lhs.at[v // 2], window11(prods), (128 * (v % 2), 256 + 128 * (v % 2)))
        for p in range(SRC // 2):
            total = jnp.dot(lhs[p, :, 0:256], rt[...], preferred_element_type=f32)
            total += jnp.dot(lhs[p, :, 256:512], rt[...], preferred_element_type=f32)
            total += jnp.dot(lx[...], rx3[p], preferred_element_type=f32)
            yy[p] = total
        for i in range(SEG):
            rows = slice(8 * i, 8 * i + 8)
            acc = None
            sub = None
            for v in range(SRC):
                y = yy[v // 2, rows, 128 * (v % 2):128 * (v % 2) + 128]
                a = y * av[v + 1, begins[v] + i]
                s = bv[v + 1, begins[v] + i]
                acc = a if acc is None else acc + a
                sub = s if sub is None else sub + s
            vol[l, i] = av[0, i] * (acc - bv[0, i] * sub)
        return carry

    lax.fori_loop(0, LEVELS, level, 0)

    def pick(i, carry):
        rows = pl.ds(pl.multiple_of(8 * i, 8), 8)
        ht = ht_out[rows, :]
        centre = up[rows, :]
        num = jnp.zeros((8, 128), f32)
        den = jnp.zeros((8, 128), f32)
        for k in range(HYP):
            table = [vol[l, i] for l in range(LEVELS)]
            for bit in range(4):
                odd = (ht & jnp.int32((1 << (4 * k + bit)) - (1 << 32 if 4 * k + bit == 31 else 0))) != 0
                table = [jnp.where(odd, table[t + 1], table[t]) for t in range(0, len(table), 2)]
            sel = 10.0 * table[0] - 10.0
            sel_out[k, rows, :] = sel
            cand = (lax.shift_right_logical(ht, 4 * k) & 15).astype(f32)
            d = cand - centre
            w = jnp.exp(sel - 0.1 * (d * d))
            num += w * cand
            den += w
        red_out[rows, :] = num / den
        return carry

    lax.fori_loop(0, SEG, pick, 0)


def score(ids, xm, xh, hyp, up):
    vmem = pl.BlockSpec(memory_space=pltpu.VMEM)
    n = SEG * 8
    return pl.pallas_call(
        score_kernel,
        out_shape=(
            jax.ShapeDtypeStruct((HYP, n, 128), f32),
            jax.ShapeDtypeStruct((n, 128), jnp.int32),
            jax.ShapeDtypeStruct((n, 128), f32),
        ),
        in_specs=[pl.BlockSpec(memory_space=pltpu.SMEM)] + [vmem] * 4,
        out_specs=(vmem,) * 3,
        scratch_shapes=[
            pltpu.VMEM((SRC + 1, NJ, 8, 128), f32),
            pltpu.VMEM((2, NJ, 8, 128), f32),
            pltpu.VMEM((256, 256), bf16),
            pltpu.VMEM((2, 256, 256), bf16),
            pltpu.VMEM((SRC, 256, 256), bf16),
            pltpu.VMEM((NM * 8 + 8, 768), bf16),
            pltpu.VMEM((NM * 8 + 8, 768), bf16),
            pltpu.VMEM((NM * 8, 256), f32),
            pltpu.VMEM((SRC + 1, NM, 8, 128), f32),
            pltpu.VMEM((SRC + 1, NM, 8, 128), f32),
            pltpu.VMEM((2, n, 512), bf16),
            pltpu.VMEM((n, 256), bf16),
            pltpu.VMEM((2, n, 256), f32),
            pltpu.VMEM((LEVELS, SEG, 8, 128), f32),
            pltpu.VMEM((COLS, ROWS), jnp.int32),
        ],
    )(ids, xm, xh, hyp, up)


def border_lanes(red):
    lane = lax.broadcasted_iota(jnp.int32, (8, 128), 1)
    out = jnp.zeros((8, 128), f32)
    for i in range(SEG):
        v = red[8 * i:8 * i + 8, :]
        out = jnp.where(lane == i, jnp.broadcast_to(v[:, 0:1], (8, 128)), out)
        out = jnp.where(lane == SEG + i, jnp.broadcast_to(v[:, 127:128], (8, 128)), out)
    return out


def black_kernel(sel, ht, red, up, above, below, left, right, out, tmp):
    row_index = lax.axis_index("row")
    col_index = lax.axis_index("col")
    row_count = lax.axis_size("row")
    col_count = lax.axis_size("col")
    lane = lax.broadcasted_iota(jnp.int32, (8, 128), 1)
    seg = lax.broadcasted_iota(jnp.int32, (8, 128), 0)
    row_edge = jnp.where((lane == 0) & (row_index == 0), 1.0, 0.0) + jnp.where(
        (lane == ROWS - 1) & (row_index == row_count - 1), 1.0, 0.0)
    above_v = above[...]
    below_v = below[...]
    for i in range(SEG):
        rows = slice(8 * i, 8 * i + 8)
        r = red[rows, :]
        u = up[rows, :]
        h = ht[rows, :]
        north = jnp.where(lane == 0, jnp.broadcast_to(above_v[:, SEG + i:SEG + i + 1], (8, 128)), pltpu.roll(r, 1, 1))
        south = jnp.where(lane == ROWS - 1, jnp.broadcast_to(below_v[:, i:i + 1], (8, 128)), pltpu.roll(r, ROWS - 1, 1))
        if i == 0:
            west = jnp.concatenate([left[7:8, :], red[8 * SEG - 8:8 * SEG - 1, :]], axis=0)
        else:
            west = red[8 * i - 8:8 * i, :]
        if i == SEG - 1:
            east = jnp.concatenate([red[1:8, :], right[0:1, :]], axis=0)
        else:
            east = red[8 * i + 8:8 * i + 16, :]
        count = 4.0 - row_edge
        if i == 0:
            count = count - jnp.where((seg == 0) & (col_index == 0), 1.0, 0.0)
        if i == SEG - 1:
            count = count - jnp.where((seg == 7) & (col_index == col_count - 1), 1.0, 0.0)
        centre = 0.5 * u + 0.5 * (north + south + west + east) / count
        num = jnp.zeros((8, 128), f32)
        den = jnp.zeros((8, 128), f32)
        for k in range(HYP):
            cand = (lax.shift_right_logical(h, 4 * k) & 15).astype(f32)
            d = cand - centre
            w = jnp.exp(sel[k, rows, :] - 0.1 * (d * d))
            num += w * cand
            den += w
        even = ((lane + i) & 1) == 0
        tmp[pl.ds(i, SEGS, stride=SEG), :] = jnp.where(even, r, num / den)
    out[...] = tmp[...].T


def blacken(sel, ht, red, up, above, below, left, right):
    vmem = pl.BlockSpec(memory_space=pltpu.VMEM)
    return pl.pallas_call(
        black_kernel,
        out_shape=jax.ShapeDtypeStruct((ROWS, COLS), f32),
        in_specs=[vmem] * 8,
        out_specs=vmem,
        scratch_shapes=[pltpu.VMEM((COLS, ROWS), f32)],
    )(sel, ht, red, up, above, below, left, right)


def shifted(array, axis, step):
    size = lax.axis_size(axis)
    pairs = [(i, i + step) for i in range(size) if 0 <= i + step < size]
    return lax.ppermute(array, axis, pairs)


def interp_matrix(fine_pos, coarse_start, coarse_pixel_number, coarse_total):
    numerator = 2 * fine_pos + 1 - UPS
    lower = numerator // (2 * UPS)
    fraction = (numerator - lower * 2 * UPS).astype(f32) / (2.0 * UPS)
    low_index = jnp.clip(lower, 0, coarse_total - 1) - coarse_start
    high_index = jnp.clip(lower + 1, 0, coarse_total - 1) - coarse_start
    columns = jnp.arange(coarse_pixel_number, dtype=jnp.int32)
    low_part = jnp.where(columns[None, :] == low_index[:, None], 1.0 - fraction[:, None], 0.0)
    high_part = jnp.where(columns[None, :] == high_index[:, None], fraction[:, None], 0.0)
    return low_part + high_part


def jacobi_step(line_span, disp, conf):
    col_pad = jnp.pad(line_span[1:-1], ((0, 0), (1, 1)))
    neighbours = line_span[:-2] + line_span[2:] + col_pad[:, :-2] + col_pad[:, 2:]
    return (conf * disp + neighbours) / (conf + 4.0)


def upsample(coarse_disp, coarse_conf):
    row_index = lax.axis_index("row")
    col_index = lax.axis_index("col")
    coarse_tile = ROWS // UPS
    disp = lax.all_gather(coarse_disp, "col", axis=0, tiled=True)
    conf = lax.all_gather(coarse_conf, "col", axis=0, tiled=True)
    height, width = disp.shape
    current = disp
    for _ in range(CITER):
        current = jacobi_step(jnp.pad(current, ((1, 1), (0, 0))), disp, conf)
    spread = jnp.pad(current, ((1, 1), (0, 0)))
    piece = lax.dynamic_slice_in_dim(spread, row_index * coarse_tile, coarse_tile + 2, 0)
    row_mat = interp_matrix(row_index * ROWS + jnp.arange(ROWS, dtype=jnp.int32),
                            row_index * coarse_tile - 1, coarse_tile + 2, height)
    order = jnp.arange(COLS, dtype=jnp.int32)
    order = (order % SEGS) * SEG + order // SEGS
    col_mat = interp_matrix(col_index * COLS + order, 0, width, width)
    high = lax.Precision.HIGHEST
    return jnp.dot(col_mat, jnp.dot(row_mat, piece, precision=high).T, precision=high)


def spread_tiles(reference_image, source_images):
    stacked = jnp.concatenate([reference_image[None], source_images], 0)
    above = shifted(stacked[:, ROWS - R:, :], "row", 1)
    below = shifted(stacked[:, :R, :], "row", -1)
    tall = jnp.concatenate([stacked, above, below], 1)
    west = shifted(tall[:, :, COLS - LEFT:], "col", 1)
    east = shifted(tall[:, :, :8], "col", -1)
    wide = jnp.concatenate([west, tall, east], 2)
    wide = jnp.pad(wide, ((0, 0), (0, 0), (PADL - LEFT, 0)))
    turned = jnp.transpose(wide, (0, 2, 1))
    main = turned[:, :, :ROWS]
    edge = turned[:, :, ROWS:]
    ref = jnp.concatenate([edge[0]] * SRC, 1)
    src = jnp.concatenate([edge[v + 1] for v in range(SRC)], 1)
    edges = jnp.pad(jnp.stack([ref, src]), ((0, 0), (0, 0), (0, 128 - SRC * HL)))
    return main, edges


def on_device(reference_image, source_images, hypotheses, source_ids, coarse_disp, coarse_conf):
    up = upsample(coarse_disp, coarse_conf)
    main, edges = spread_tiles(reference_image, source_images)
    sel, ht, red = score(source_ids, main, edges, hypotheses, up)
    border = border_lanes(red)
    above = shifted(border, "row", 1)
    below = shifted(border, "row", -1)
    left = shifted(red[8 * SEG - 8:], "col", 1)
    right = shifted(red[:8], "col", -1)
    return blacken(sel, ht, red, up, above, below, left, right)


def solution(mesh):
    in_specs = (
        P("row", "col"),
        P(None, "row", "col"),
        P(None, "row", "col"),
        P(),
        P("col", None),
        P("col", None),
    )
    return jax.shard_map(
        on_device, mesh=mesh, in_specs=in_specs, out_specs=P("row", "col"), check_vma=False
    )
```

time: 320 us -> 227 us (0.71)
  the two profiles are of different devices: /device:TPU:229 before, /device:TPU:33 now
where the time goes in v1:
time: 227 us
  waiting for transfers between devices  128 us (56%)
  starting transfers between devices  37.8 us (17%)
  Pallas kernels  25.5 us (11%)
  between operations  13.9 us (6%)
  local copies, waits for them, and re-layouts  12 us (5%)
  other arithmetic  7.63 us (3%)
    all_gather x1, waiting for transfers between devices, upsample(): conf = lax.all_gather(coarse_conf, 'col', axis=0, tiled=True)  79.2 us
    ppermute x8, starting transfers between devices, shifted(): return lax.ppermute(array, axis, pairs)  37.8 us
    all_gather x1, waiting for transfers between devices, upsample(): disp = lax.all_gather(coarse_disp, 'col', axis=0, tiled=True)  37.7 us
    pallas_call x1, Pallas kernels, score(): pl.pallas_call(score_kernel, out_shape=(jax.ShapeDtypeStruct((HYP, n, 128...  22.7 us
    ppermute x8, waiting for transfers between devices, shifted(): return lax.ppermute(array, axis, pairs)  10.6 us
    div x4, other arithmetic, jacobi_step(): return (conf * disp + neighbours) / (conf + 4.0)  6.4 us
  transfers between devices with their start and end apart: 10, of which 5 were waited for; matrix products, arithmetic and copies ran while one was open for 3% of the time, Pallas kernels for 0%

profile of v1, /device:TPU:33, one launch (start us, length us, event | category | flops | bytes accessed | tf_op | source)
XLA Modules:
  0.0 226.7 jit_solution(5873086297927639954)
XLA Ops:
  6.5 0.7 all-gather.5.cloned.1.call-update
  7.3 1.0 copy.11
  8.3 1.2 copy.12
  9.5 0.2 slice_maximum_fusion
  9.8 0.2 copy.14
  10.0 2.6 %collective-permute-start.1 = (f32[5,5,256]{2,1,0:T(8,128)S(1)}, f32[5,5,256]{2,1,0:T(8,128)S(1)}, u32[]{:S(2)}, u32[]{:S(2)}) collective-permute-start(f32[5,5,256]{2,1,0:T(8,128)S(1)} %copy.14), channel_id=1, source_target_pairs={{16,0},{32,16},{48,32},{64,48},{80,64},{96,80},{112,96},{128,112},... | collective-permute-start | bytes 76808 | tf_op jit(solution)/shard_map/ppermute | solution.py:325
  12.6 0.2 copy.13
  12.8 4.6 %collective-permute-start = (f32[5,5,256]{2,1,0:T(8,128)S(1)}, f32[5,5,256]{2,1,0:T(8,128)S(1)}, u32[]{:S(2)}, u32[]{:S(2)}) collective-permute-start(f32[5,5,256]{2,1,0:T(8,128)S(1)} %copy.13), channel_id=1, source_target_pairs={{0,16},{16,32},{32,48},{48,64},{64,80},{80,96},{96,112},{112,128},... | collective-permute-start | bytes 76808 | tf_op jit(solution)/shard_map/ppermute | solution.py:325
  17.9 0.6 collective-permute-done
  18.5 0.3 copy.15
  18.7 0.3 copy.16
  19.0 0.1 pad_maximum_fusion.1
  19.1 3.1 %collective-permute-start.2 = (f32[5,138,50]{1,2,0:T(8,128)S(1)}, f32[5,138,50]{1,2,0:T(8,128)S(1)}, u32[]{:S(2)}, u32[]{:S(2)}) collective-permute-start(f32[5,138,50]{1,2,0:T(8,128)S(1)} %pad_maximum_fusion.1), channel_id=1, source_target_pairs={{0,1},{1,2},{2,3},{3,4},{4,5},{5,6},{6,7},{7,8},{8,9},{9,10},{10,1... | collective-permute-start | bytes 414008 | tf_op jit(solution)/shard_map/ppermute | solution.py:325
  22.2 0.1 pad_maximum_fusion.3
  22.3 4.3 %collective-permute-start.3 = (f32[5,138,8]{1,2,0:T(8,128)S(1)}, f32[5,138,8]{1,2,0:T(8,128)S(1)}, u32[]{:S(2)}, u32[]{:S(2)}) collective-permute-start(f32[5,138,8]{1,2,0:T(8,128)S(1)} %pad_maximum_fusion.3), channel_id=1, source_target_pairs={{1,0},{2,1},{3,2},{4,3},{5,4},{6,5},{7,6},{8,7},{9,8},{10,9},{11,1... | collective-permute-start | bytes 66248 | tf_op jit(solution)/shard_map/ppermute | solution.py:325
  26.6 6.0 %collective-permute-done.3 = f32[5,138,8]{1,2,0:T(8,128)S(1)} collective-permute-done((f32[5,138,8]{1,2,0:T(8,128)S(1)}, f32[5,138,8]{1,2,0:T(8,128)S(1)}, u32[]{:S(2)}, u32[]{:S(2)}) %collective-permute-start.3) | collective-permute-done | bytes 22112 | tf_op jit(solution)/shard_map/ppermute | solution.py:325
  32.6 0.3 fusion
  32.9 1.0 slice.476.xm
  33.9 0.1 slice_bitcast_fusion.4
  33.9 0.1 copy.17
  34.0 0.1 copy.24
  34.1 0.1 copy.23
  34.3 0.1 copy.22
  34.4 0.1 copy.21
  34.6 0.1 copy.25
  34.7 0.8 pad.38.xh
  35.5 37.7 %all-gather.5.cloned.1.call-done = f32[512,512]{1,0:T(8,128)} async-done(((f32[32,512]{1,0:T(8,128)}), f32[512,512]{1,0:T(8,128)}) %all-gather.5.cloned.1.call-update) | async-done | bytes 1048592 | tf_op jit(solution)/shard_map/all_gather | solution.py:350
  73.2 79.2 %all-gather.3.cloned.1.call-done = f32[512,512]{1,0:T(8,128)} async-done(((f32[32,512]{1,0:T(8,128)}), f32[512,512]{1,0:T(8,128)}) %all-gather.3.cloned.1.call-update) | async-done | bytes 1048592 | tf_op jit(solution)/shard_map/all_gather | solution.py:351
  152.3 4.4 %fusion.11 = (f32[512,512]{1,0:T(8,128)S(1)}, f32[512,512]{1,0:T(8,128)S(1)}) fusion(f32[512,512]{1,0:T(8,128)} %all-gather.5.cloned.1.call-done, f32[512,512]{1,0:T(8,128)} %all-gather.3.cloned.1.call-done), kind=kLoop, calls=%fused_computation.23 | loop fusion | flops 1835008 | bytes 4194304 | tf_op jit(solution)/shard_map/div | solution.py:343
  156.8 0.6 fusion.15
  157.5 0.7 fusion.19
  158.1 0.7 fusion.23
  158.8 0.4 fusion.33
  159.2 1.4 fusion.24.up
  160.6 22.7 %shard_map.64 = (f32[8,256,128]{2,1,0:T(8,128)}, s32[256,128]{1,0:T(8,128)}, f32[256,128]{1,0:T(8,128)}) custom-call(s32[4]{0:T(128)} %ids.1, f32[5,320,128]{2,1,0:T(8,128)} %slice.476.xm, f32[2,320,128]{2,1,0:T(8,128)} %pad.38.xh, s32[8,128,256]{2,1,0:T(8,128)} %hyp.1, f32[256,128]{1,0:T(8,128)} %fusion.24.up), custom_call_target="tpu_custom_call" | custom-call | tf_op jit(solution)/shard_map/pallas_call | solution.py:227
  183.3 1.0 slice_reduce_fusion.60
  184.3 0.7 fusion.52
  185.0 1.3 slice_reduce_fusion.61
  186.4 1.3 slice_reduce_fusion.62
  187.7 1.3 slice_reduce_fusion.63
  189.0 0.2 select_select_fusion
  189.2 13.6 %collective-permute-start.5 = (f32[8,128]{1,0:T(8,128)S(1)}, f32[8,128]{1,0:T(8,128)S(1)}, u32[]{:S(2)}, u32[]{:S(2)}) collective-permute-start(f32[8,128]{1,0:T(8,128)S(1)} %select_select_fusion), channel_id=1, source_target_pairs={{16,0},{32,16},{48,32},{64,48},{80,64},{96,80},{112,96},{128,112},... | collective-permute-start | bytes 12296 | tf_op jit(solution)/shard_map/ppermute | solution.py:325
  202.8 4.4 %collective-permute-start.4 = (f32[8,128]{1,0:T(8,128)S(1)}, f32[8,128]{1,0:T(8,128)S(1)}, u32[]{:S(2)}, u32[]{:S(2)}) collective-permute-start(f32[8,128]{1,0:T(8,128)S(1)} %select_select_fusion), channel_id=1, source_target_pairs={{0,16},{16,32},{32,48},{48,64},{64,80},{80,96},{96,112},{112,128},... | collective-permute-start | bytes 12296 | tf_op jit(solution)/shard_map/ppermute | solution.py:325
  207.2 2.9 %collective-permute-start.7 = (f32[8,128]{1,0:T(8,128)S(1)}, f32[8,128]{1,0:T(8,128)S(1)}, u32[]{:S(2)}, u32[]{:S(2)}) collective-permute-start(f32[8,128]{1,0:T(8,128)S(1)} %get-tuple-element.84), channel_id=1, source_target_pairs={{1,0},{2,1},{3,2},{4,3},{5,4},{6,5},{7,6},{8,7},{9,8},{10,9},{11,1... | collective-permute-start | bytes 12296 | tf_op jit(solution)/shard_map/ppermute | solution.py:325
  210.1 2.4 %collective-permute-start.6 = (f32[8,128]{1,0:T(8,128)S(1)}, f32[8,128]{1,0:T(8,128)S(1)}, u32[]{:S(2)}, u32[]{:S(2)}) collective-permute-start(f32[8,128]{1,0:T(8,128)S(1)} %get-tuple-element.85), channel_id=1, source_target_pairs={{0,1},{1,2},{2,3},{3,4},{4,5},{5,6},{6,7},{7,8},{8,9},{9,10},{10,1... | collective-permute-start | bytes 12296 | tf_op jit(solution)/shard_map/ppermute | solution.py:325
  212.6 4.0 %collective-permute-done.6.left = f32[8,128]{1,0:T(8,128)S(1)} collective-permute-done((f32[8,128]{1,0:T(8,128)S(1)}, f32[8,128]{1,0:T(8,128)S(1)}, u32[]{:S(2)}, u32[]{:S(2)}) %collective-permute-start.6) | collective-permute-done | bytes 4128 | tf_op jit(solution)/shard_map/ppermute | solution.py:325
  216.6 0.6 copy-done.4
  217.1 2.7 %shard_map.65 = f32[128,256]{1,0:T(8,128)} custom-call(f32[8,256,128]{2,1,0:T(8,128)} %get-tuple-element.8.sel, s32[256,128]{1,0:T(8,128)} %get-tuple-element.9.ht, f32[256,128]{1,0:T(8,128)} %get-tuple-element.10.red, f32[256,128]{1,0:T(8,128)} %fusion.24.up, f32[8,128]{1,0:T(8,128)} %copy-done.2, f32[8,128]{1,0:T(8,128)} %copy-done.1, f32[8,128]{1,0:T(8,128)} %copy-done.4, ...), custom_call_target="tpu_custom_call" | custom-call | tf_op jit(solution)/shard_map/pallas_call | solution.py:313
  (55 shorter events, 0.4 us)
Async XLA Ops:
  6.5 66.6 %all-gather.5.cloned.1.call-start = ((), (), s32[]{:S(2)}) async-start(), calls=%async_computation.1 | async-start | bytes 1114112 | tf_op jit(solution)/shard_map/all_gather | solution.py:350
  7.3 145.1 %all-gather.3.cloned.1.call-start = ((), (), s32[]{:S(2)}) async-start(), calls=%async_computation | async-start | bytes 1114112 | tf_op jit(solution)/shard_map/all_gather | solution.py:351
  10.0 8.7 %collective-permute-start.1 = (f32[5,5,256]{2,1,0:T(8,128)S(1)}, f32[5,5,256]{2,1,0:T(8,128)S(1)}, u32[]{:S(2)}, u32[]{:S(2)}) collective-permute-start(f32[5,5,256]{2,1,0:T(8,128)S(1)} %copy.14), channel_id=1, source_target_pairs={{16,0},{32,16},{48,32},{64,48},{80,64},{96,80},{112,96},{128,112},... | collective-permute-start | bytes 76808 | tf_op jit(solution)/shard_map/ppermute | solution.py:325
  12.8 5.6 %collective-permute-start = (f32[5,5,256]{2,1,0:T(8,128)S(1)}, f32[5,5,256]{2,1,0:T(8,128)S(1)}, u32[]{:S(2)}, u32[]{:S(2)}) collective-permute-start(f32[5,5,256]{2,1,0:T(8,128)S(1)} %copy.13), channel_id=1, source_target_pairs={{0,16},{16,32},{32,48},{48,64},{64,80},{80,96},{96,112},{112,128},... | collective-permute-start | bytes 76808 | tf_op jit(solution)/shard_map/ppermute | solution.py:325
  19.1 13.5 %collective-permute-start.2 = (f32[5,138,50]{1,2,0:T(8,128)S(1)}, f32[5,138,50]{1,2,0:T(8,128)S(1)}, u32[]{:S(2)}, u32[]{:S(2)}) collective-permute-start(f32[5,138,50]{1,2,0:T(8,128)S(1)} %pad_maximum_fusion.1), channel_id=1, source_target_pairs={{0,1},{1,2},{2,3},{3,4},{4,5},{5,6},{6,7},{7,8},{8,9},{9,10},{10,1... | collective-permute-start | bytes 414008 | tf_op jit(solution)/shard_map/ppermute | solution.py:325
  22.3 10.4 %collective-permute-start.3 = (f32[5,138,8]{1,2,0:T(8,128)S(1)}, f32[5,138,8]{1,2,0:T(8,128)S(1)}, u32[]{:S(2)}, u32[]{:S(2)}) collective-permute-start(f32[5,138,8]{1,2,0:T(8,128)S(1)} %pad_maximum_fusion.3), channel_id=1, source_target_pairs={{1,0},{2,1},{3,2},{4,3},{5,4},{6,5},{7,6},{8,7},{9,8},{10,9},{11,1... | collective-permute-start | bytes 66248 | tf_op jit(solution)/shard_map/ppermute | solution.py:325
  152.3 4.5 %copy-start = (f32[512,512]{1,0:T(8,128)S(1)}, f32[512,512]{1,0:T(8,128)}, u32[]{:S(2)}) copy-start(f32[512,512]{1,0:T(8,128)} %all-gather.3.cloned.1.call-done) | copy-start | bytes 3145732
  189.2 23.3 %collective-permute-start.5 = (f32[8,128]{1,0:T(8,128)S(1)}, f32[8,128]{1,0:T(8,128)S(1)}, u32[]{:S(2)}, u32[]{:S(2)}) collective-permute-start(f32[8,128]{1,0:T(8,128)S(1)} %select_select_fusion), channel_id=1, source_target_pairs={{16,0},{32,16},{48,32},{64,48},{80,64},{96,80},{112,96},{128,112},... | collective-permute-start | bytes 12296 | tf_op jit(solution)/shard_map/ppermute | solution.py:325
  202.8 9.7 %collective-permute-start.4 = (f32[8,128]{1,0:T(8,128)S(1)}, f32[8,128]{1,0:T(8,128)S(1)}, u32[]{:S(2)}, u32[]{:S(2)}) collective-permute-start(f32[8,128]{1,0:T(8,128)S(1)} %select_select_fusion), channel_id=1, source_target_pairs={{0,16},{16,32},{32,48},{48,64},{64,80},{80,96},{96,112},{112,128},... | collective-permute-start | bytes 12296 | tf_op jit(solution)/shard_map/ppermute | solution.py:325
  207.2 5.3 %collective-permute-start.7 = (f32[8,128]{1,0:T(8,128)S(1)}, f32[8,128]{1,0:T(8,128)S(1)}, u32[]{:S(2)}, u32[]{:S(2)}) collective-permute-start(f32[8,128]{1,0:T(8,128)S(1)} %get-tuple-element.84), channel_id=1, source_target_pairs={{1,0},{2,1},{3,2},{4,3},{5,4},{6,5},{7,6},{8,7},{9,8},{10,9},{11,1... | collective-permute-start | bytes 12296 | tf_op jit(solution)/shard_map/ppermute | solution.py:325
  210.1 6.5 %collective-permute-start.6 = (f32[8,128]{1,0:T(8,128)S(1)}, f32[8,128]{1,0:T(8,128)S(1)}, u32[]{:S(2)}, u32[]{:S(2)}) collective-permute-start(f32[8,128]{1,0:T(8,128)S(1)} %get-tuple-element.85), channel_id=1, source_target_pairs={{0,1},{1,2},{2,3},{3,4},{4,5},{5,6},{6,7},{7,8},{8,9},{9,10},{10,1... | collective-permute-start | bytes 12296 | tf_op jit(solution)/shard_map/ppermute | solution.py:325
  212.5 4.0 %copy-start.1 = (f32[8,128]{1,0:T(8,128)}, f32[8,128]{1,0:T(8,128)S(1)}, u32[]{:S(2)}) copy-start(f32[8,128]{1,0:T(8,128)S(1)} %collective-permute-done.5.below) | copy-start | bytes 12292
  212.5 4.0 %copy-start.2 = (f32[8,128]{1,0:T(8,128)}, f32[8,128]{1,0:T(8,128)S(1)}, u32[]{:S(2)}) copy-start(f32[8,128]{1,0:T(8,128)S(1)} %collective-permute-done.4.above) | copy-start | bytes 12292
  212.6 4.0 %copy-start.3 = (f32[8,128]{1,0:T(8,128)}, f32[8,128]{1,0:T(8,128)S(1)}, u32[]{:S(2)}) copy-start(f32[8,128]{1,0:T(8,128)S(1)} %collective-permute-done.7.right) | copy-start | bytes 12292
  216.6 0.6 copy-start.4
Sparse Core Ops, SparseCore 0:
  9.4 63.7 all-gather.4
  75.2 77.0 all-gather.2

commit v2 on v1

--- a/solution.py
+++ b/solution.py
@@ -86,8 +86,240 @@
     return jnp.where(good, 1.0, 0.0).astype(bf16)
 
 
-def score_kernel(ids, xm, xh, hyp, up, sel_out, ht_out, red_out,
-                 xs, hs, rt, rx3, rmom, xmom, lmom, cmom, av, bv, lhs, lx, yy, vol, htc):
+MESH = pl.DeviceIdType.MESH
+
+
+def exchange_kernel(ref, src, hyp, disp, conf, xm, href, hsrc, cb, ht, htc, send, recv, local):
+    row, col = lax.axis_index("row"), lax.axis_index("col")
+    nr, nc = lax.axis_size("row"), lax.axis_size("col")
+    wide = cb.shape[2]
+    last = (disp.shape[1] - wide) // 128
+
+    def inside(dr, dc):
+        good = row >= 0
+        if dr:
+            good = good & ((row > 0) if dr < 0 else (row < nr - 1))
+        if dc:
+            good = good & ((col > 0) if dc < 0 else (col < nc - 1))
+        return good
+
+    def away(dr, dc):
+        return {"row": lax.rem(row + dr + nr, nr), "col": lax.rem(col + dc + nc, nc)}
+
+    def tile(j):
+        return pl.ds(pl.multiple_of(128 * jnp.clip((32 * j - 32 + 27) // 128, 0, last), 128), wide)
+
+    around = [(dr, dc) for dr in (-1, 0, 1) for dc in (-1, 0, 1) if dr or dc]
+
+    par, home = row // nc, lax.rem(row, nc)
+    main_to = {"row": 2 * col + par, "col": home}
+    main_from = {"row": nc * lax.rem(row, 2) + col, "col": row // 2}
+    own = (2 * col + par == row) & (home == col)
+    other = jnp.logical_not(own)
+    side_to_row = 2 * col + 2 - 3 * par
+    side_sends = (side_to_row >= 0) & (side_to_row < nr)
+    side_to = {"row": jnp.clip(side_to_row, 0, nr - 1), "col": home}
+    odd = lax.rem(row, 2)
+    side_col = row // 2 - 1 + 2 * odd
+    side_comes = (side_col >= 0) & (side_col < nc)
+    side_from = {"row": nc * odd + col, "col": jnp.clip(side_col, 0, nc - 1)}
+
+    barrier = pltpu.get_barrier_semaphore()
+    expected = jnp.int32(0)
+    for dr, dc in around:
+        expected += inside(dr, dc).astype(jnp.int32)
+
+        @pl.when(inside(dr, dc))
+        def _(dr=dr, dc=dc):
+            pl.semaphore_signal(barrier, inc=1, device_id=away(dr, dc), device_id_type=MESH)
+
+    @pl.when(other)
+    def _():
+        pl.semaphore_signal(barrier, inc=1, device_id=main_from, device_id_type=MESH)
+
+    @pl.when(side_comes)
+    def _():
+        pl.semaphore_signal(barrier, inc=1, device_id=side_from, device_id_type=MESH)
+
+    expected += other.astype(jnp.int32) + side_sends.astype(jnp.int32)
+    pl.semaphore_wait(barrier, expected)
+
+    copies = []
+
+    def push(dr, dc, source, target):
+        n = len(copies)
+        copy = pltpu.make_async_remote_copy(source, target, send.at[n], recv.at[n], device_id=away(dr, dc), device_id_type=MESH)
+        copies.append((dr, dc, copy, target))
+
+        @pl.when(inside(dr, dc))
+        def _():
+            copy.start()
+
+    for dr in (1, -1):
+        here = pl.ds(ROWS - 8, 8) if dr == 1 else pl.ds(0, 8)
+        side = 0 if dr == 1 else 1
+        for dc in (1, -1, 0):
+            lanes = {0: (0, COLS), 1: (COLS - 128, 128), -1: (0, 128)}[dc]
+            to = {0: 128, 1: 0, -1: 384}[dc]
+            push(dr, dc, src.at[:, here, pl.ds(*lanes)], hsrc.at[side, :, :, pl.ds(to, lanes[1])])
+            push(dr, dc, ref.at[here, pl.ds(*lanes)], href.at[side, :, pl.ds(to, lanes[1])])
+
+    coarse = []
+    for m, array in enumerate((disp, conf)):
+        main_src = array.at[pl.ds(pl.multiple_of(8 * par, 8), 24), tile(home)]
+        main_dst = cb.at[m, pl.ds(pl.multiple_of(8 - 8 * par, 8), 24), :]
+        side_src = array.at[pl.ds(pl.multiple_of(24 - 24 * par, 8), 8), tile(home)]
+        side_dst = cb.at[m, pl.ds(pl.multiple_of(24 * par, 8), 8), :]
+        n = 20 + 2 * m
+        main = pltpu.make_async_remote_copy(main_src, main_dst, send.at[n], recv.at[n], device_id=main_to, device_id_type=MESH)
+        mine = pltpu.make_async_copy(main_src, main_dst, local.at[m])
+        rest = pltpu.make_async_remote_copy(side_src, side_dst, send.at[n + 1], recv.at[n + 1], device_id=side_to, device_id_type=MESH)
+        main_in = cb.at[m, pl.ds(pl.multiple_of(8 - 8 * odd, 8), 24), :]
+        side_in = cb.at[m, pl.ds(pl.multiple_of(24 * odd, 8), 8), :]
+        got_main = pltpu.make_async_remote_copy(main_src, main_in, send.at[n], recv.at[n], device_id=main_to, device_id_type=MESH)
+        got_side = pltpu.make_async_remote_copy(side_src, side_in, send.at[n + 1], recv.at[n + 1], device_id=side_to, device_id_type=MESH)
+        coarse.append((main, mine, rest, got_main, got_side, side_in))
+
+        @pl.when(other)
+        def _(main=main):
+            main.start()
+
+        @pl.when(own)
+        def _(mine=mine):
+            mine.start()
+
+        @pl.when(side_sends)
+        def _(rest=rest):
+            rest.start()
+
+    for v in range(SRC):
+        xm[v + 1, PADL:PADL + COLS, :] = src[v].T
+    xm[0, PADL:PADL + COLS, :] = ref[...].T
+    push(0, 1, xm.at[pl.ds(1, SRC), pl.ds(COLS, PADL), :], xm.at[pl.ds(1, SRC), pl.ds(0, PADL), :])
+    push(0, 1, xm.at[pl.ds(0, 1), pl.ds(PADL + COLS - 8, 8), :], xm.at[pl.ds(0, 1), pl.ds(PADL - 8, 8), :])
+    push(0, -1, xm.at[:, pl.ds(PADL, 8), :], xm.at[:, pl.ds(PADL + COLS, 8), :])
+
+    packed = hyp[0]
+    for k in range(1, HYP):
+        packed = packed | (hyp[k] << (4 * k))
+    htc[...] = packed.T
+    for i in range(SEG):
+        ht[8 * i:8 * i + 8, :] = htc[pl.ds(i, SEGS, stride=SEG), :]
+
+    for dr, dc, copy, target in copies:
+        @pl.when(inside(-dr, -dc))
+        def _(copy=copy):
+            copy.wait_recv()
+
+        @pl.when(jnp.logical_not(inside(-dr, -dc)))
+        def _(target=target):
+            target[...] = jnp.zeros(target.shape, f32)
+
+    for main, mine, rest, got_main, got_side, side_in in coarse:
+        @pl.when(other)
+        def _(got_main=got_main):
+            got_main.wait_recv()
+
+        @pl.when(own)
+        def _(mine=mine):
+            mine.wait()
+
+        @pl.when(side_comes)
+        def _(got_side=got_side):
+            got_side.wait_recv()
+
+        @pl.when(jnp.logical_not(side_comes))
+        def _(side_in=side_in):
+            side_in[...] = jnp.zeros(side_in.shape, f32)
+
+        @pl.when(other)
+        def _(main=main):
+            main.wait_send()
+
+        @pl.when(side_sends)
+        def _(rest=rest):
+            rest.wait_send()
+
+    for dr, dc, copy, target in copies:
+        @pl.when(inside(dr, dc))
+        def _(copy=copy):
+            copy.wait_send()
+
+
+def exchange(ref, src, hyp, disp, conf):
+    vmem = pl.BlockSpec(memory_space=pltpu.VMEM)
+    wide = min(256, disp.shape[1])
+    return pl.pallas_call(
+        exchange_kernel,
+        out_shape=(
+            jax.ShapeDtypeStruct((SRC + 1, CI, 128), f32),
+            jax.ShapeDtypeStruct((2, 8, 512), f32),
+            jax.ShapeDtypeStruct((2, SRC, 8, 512), f32),
+            jax.ShapeDtypeStruct((2, 32, wide), f32),
+            jax.ShapeDtypeStruct((COLS, 128), jnp.int32),
+        ),
+        in_specs=[vmem] * 5,
+        out_specs=(vmem,) * 5,
+        scratch_shapes=[
+            pltpu.VMEM((COLS, ROWS), jnp.int32),
+            pltpu.SemaphoreType.DMA((24,)),
+            pltpu.SemaphoreType.DMA((24,)),
+            pltpu.SemaphoreType.DMA((2,)),
+        ],
+        compiler_params=pltpu.CompilerParams(collective_id=0, has_side_effects=True),
+    )(ref, src, hyp, disp, conf)
+
+
+def interp_block(fine, coarse_start, total, shape):
+    numerator = 2 * fine + 1 - UPS
+    lower = numerator >> 4
+    fraction = (numerator - lower * 2 * UPS).astype(f32) / (2.0 * UPS)
+    where = lax.broadcasted_iota(jnp.int32, shape, 1) + coarse_start
+    low = jnp.where(where == jnp.clip(lower, 0, total - 1), 1.0 - fraction, 0.0)
+    high = jnp.where(where == jnp.clip(lower + 1, 0, total - 1), fraction, 0.0)
+    return low + high
+
+
+def upsampled_tile(cb, total_rows, total_cols):
+    row, col = lax.axis_index("row"), lax.axis_index("col")
+    high, wide = cb.shape[1:]
+    start = 16 * row - 8
+    begin = 128 * jnp.clip((32 * col - 32 + 27) // 128, 0, (total_cols - wide) // 128)
+    disp, conf = cb[0], cb[1]
+    place = lax.broadcasted_iota(jnp.int32, (high, wide), 0) + start
+    lane = lax.broadcasted_iota(jnp.int32, (high, wide), 1)
+    good = (place >= 0) & (place < total_rows)
+    local = lax.broadcasted_iota(jnp.int32, (high, wide), 0)
+    pull = conf * disp
+    current = disp
+    for _ in range(CITER):
+        up = jnp.where(local == 0, 0.0, pltpu.roll(current, 1, 0))
+        down = jnp.where(local == high - 1, 0.0, pltpu.roll(current, high - 1, 0))
+        left = jnp.where(lane == 0, 0.0, pltpu.roll(current, 1, 1))
+        right = jnp.where(lane == wide - 1, 0.0, pltpu.roll(current, wide - 1, 1))
+        current = jnp.where(good, (pull + (up + down + left + right)) / (conf + 4.0), 0.0)
+    fine_rows = row * ROWS + lax.broadcasted_iota(jnp.int32, (ROWS, high), 0)
+    order = lax.broadcasted_iota(jnp.int32, (COLS, wide), 0)
+    fine_cols = col * COLS + (order & (SEGS - 1)) * SEG + (order >> 3)
+    row_mat = interp_block(fine_rows, start, total_rows, (ROWS, high))
+    col_mat = interp_block(fine_cols, begin, total_cols, (COLS, wide))
+    best = lax.Precision.HIGHEST
+    tall = jnp.dot(row_mat, current, precision=best, preferred_element_type=f32)
+    return lax.dot_general(col_mat, tall, (((1,), (1,)), ((), ())), precision=best, preferred_element_type=f32)
+
+
+def score_kernel(coarse_shape, ids, xm, href, hsrc, cb, ht_ref, sel_out, up, red_out, lanes_out,
+                 xs, hs, rt, rx3, rmom, xmom, lmom, cmom, av, bv, lhs, lx, yy, vol, zt):
+    up[...] = upsampled_tile(cb, *coarse_shape)
+    gap = jnp.zeros((64 - SRC * HL, 512), f32)
+    stack = []
+    for v in range(SRC):
+        stack += [hsrc[0, v, 8 - R:8, :], hsrc[1, v, 0:R, :]]
+    stack.append(gap)
+    for v in range(SRC):
+        stack += [href[0, 8 - R:8, :], href[1, 0:R, :]]
+    stack.append(gap)
+    zt[...] = jnp.concatenate(stack, axis=0).T
     zero = jnp.zeros((128, 128), bf16)
     b = band_main()
     halo = [band_halo(v) for v in range(SRC)]
@@ -108,17 +340,11 @@
         rows = pl.ds(j + PADL - LEFT, SEGS, stride=SEG)
         for v in range(SRC):
             xs[v + 1, j] = xm[v + 1, rows, :]
-        hs[1, j] = xh[1, rows, :]
+        edge = zt[pl.ds(j + 128 - LEFT, SEGS, stride=SEG), :]
+        hs[1, j] = edge
         if j >= SHIFT:
             xs[0, j] = xm[0, rows, :]
-            hs[0, j] = xh[0, rows, :]
-
-    packed = hyp[0]
-    for k in range(1, HYP):
-        packed = packed | (hyp[k] << (4 * k))
-    htc[...] = packed.T
-    for i in range(SEG):
-        ht_out[8 * i:8 * i + 8, :] = htc[pl.ds(i, SEGS, stride=SEG), :]
+            hs[0, j] = pltpu.roll(edge, 64, 1)
 
     def moments(load, first, count, ref):
         vals = [load(first + j) for j in range(count)]
@@ -199,7 +425,7 @@
 
     def pick(i, carry):
         rows = pl.ds(pl.multiple_of(8 * i, 8), 8)
-        ht = ht_out[rows, :]
+        ht = ht_ref[rows, :]
         centre = up[rows, :]
         num = jnp.zeros((8, 128), f32)
         den = jnp.zeros((8, 128), f32)
@@ -221,18 +447,28 @@
     lax.fori_loop(0, SEG, pick, 0)
 
 
-def score(ids, xm, xh, hyp, up):
+    lane = lax.broadcasted_iota(jnp.int32, (8, 128), 1)
+    border = jnp.zeros((8, 128), f32)
+    for i in range(SEG):
+        v = red_out[8 * i:8 * i + 8, :]
+        border = jnp.where(lane == i, jnp.broadcast_to(v[:, 0:1], (8, 128)), border)
+        border = jnp.where(lane == SEG + i, jnp.broadcast_to(v[:, 127:128], (8, 128)), border)
+    lanes_out[...] = border
+
+
+def score(ids, xm, href, hsrc, cb, ht, coarse_shape):
     vmem = pl.BlockSpec(memory_space=pltpu.VMEM)
     n = SEG * 8
     return pl.pallas_call(
-        score_kernel,
+        functools.partial(score_kernel, coarse_shape),
         out_shape=(
             jax.ShapeDtypeStruct((HYP, n, 128), f32),
-            jax.ShapeDtypeStruct((n, 128), jnp.int32),
             jax.ShapeDtypeStruct((n, 128), f32),
+            jax.ShapeDtypeStruct((n, 128), f32),
+            jax.ShapeDtypeStruct((8, 128), f32),
         ),
-        in_specs=[pl.BlockSpec(memory_space=pltpu.SMEM)] + [vmem] * 4,
-        out_specs=(vmem,) * 3,
+        in_specs=[pl.BlockSpec(memory_space=pltpu.SMEM)] + [vmem] * 5,
+        out_specs=(vmem,) * 4,
         scratch_shapes=[
             pltpu.VMEM((SRC + 1, NJ, 8, 128), f32),
             pltpu.VMEM((2, NJ, 8, 128), f32),
@@ -248,22 +484,12 @@
             pltpu.VMEM((n, 256), bf16),
             pltpu.VMEM((2, n, 256), f32),
             pltpu.VMEM((LEVELS, SEG, 8, 128), f32),
-            pltpu.VMEM((COLS, ROWS), jnp.int32),
+            pltpu.VMEM((512, 128), f32),
         ],
-    )(ids, xm, xh, hyp, up)
-
-
-def border_lanes(red):
-    lane = lax.broadcasted_iota(jnp.int32, (8, 128), 1)
-    out = jnp.zeros((8, 128), f32)
-    for i in range(SEG):
-        v = red[8 * i:8 * i + 8, :]
-        out = jnp.where(lane == i, jnp.broadcast_to(v[:, 0:1], (8, 128)), out)
-        out = jnp.where(lane == SEG + i, jnp.broadcast_to(v[:, 127:128], (8, 128)), out)
-    return out
-
-
-def black_kernel(sel, ht, red, up, above, below, left, right, out, tmp):
+    )(ids, xm, href, hsrc, cb, ht)
+
+
+def black_kernel(sel, ht, red, up, border, out, tmp, near, send, recv):
     row_index = lax.axis_index("row")
     col_index = lax.axis_index("col")
     row_count = lax.axis_size("row")
@@ -272,8 +498,52 @@
     seg = lax.broadcasted_iota(jnp.int32, (8, 128), 0)
     row_edge = jnp.where((lane == 0) & (row_index == 0), 1.0, 0.0) + jnp.where(
         (lane == ROWS - 1) & (row_index == row_count - 1), 1.0, 0.0)
-    above_v = above[...]
-    below_v = below[...]
+    def inside(dr, dc):
+        if dr:
+            return (row_index > 0) if dr < 0 else (row_index < row_count - 1)
+        return (col_index > 0) if dc < 0 else (col_index < col_count - 1)
+
+    def away(dr, dc):
+        return {"row": lax.rem(row_index + dr + row_count, row_count),
+                "col": lax.rem(col_index + dc + col_count, col_count)}
+
+    around = [(1, 0), (-1, 0), (0, 1), (0, -1)]
+    sources = [border, border, red.at[pl.ds(8 * SEG - 8, 8), :], red.at[pl.ds(0, 8), :]]
+    barrier = pltpu.get_barrier_semaphore()
+    expected = jnp.int32(0)
+    for dr, dc in around:
+        expected += inside(dr, dc).astype(jnp.int32)
+
+        @pl.when(inside(dr, dc))
+        def _(dr=dr, dc=dc):
+            pl.semaphore_signal(barrier, inc=1, device_id=away(dr, dc), device_id_type=MESH)
+
+    pl.semaphore_wait(barrier, expected)
+    copies = []
+    for n, (dr, dc) in enumerate(around):
+        copy = pltpu.make_async_remote_copy(sources[n], near.at[n], send.at[n], recv.at[n], device_id=away(dr, dc), device_id_type=MESH)
+        copies.append(copy)
+
+        @pl.when(inside(dr, dc))
+        def _(copy=copy):
+            copy.start()
+
+    for n, (dr, dc) in enumerate(around):
+        @pl.when(inside(-dr, -dc))
+        def _(n=n):
+            copies[n].wait_recv()
+
+        @pl.when(jnp.logical_not(inside(-dr, -dc)))
+        def _(n=n):
+            near[n] = jnp.zeros((8, 128), f32)
+
+        @pl.when(inside(dr, dc))
+        def _(n=n):
+            copies[n].wait_send()
+
+    above_v = near[0]
+    below_v = near[1]
+    left, right = near.at[2], near.at[3]
     for i in range(SEG):
         rows = slice(8 * i, 8 * i + 8)
         r = red[rows, :]
@@ -308,90 +578,28 @@
     out[...] = tmp[...].T
 
 
-def blacken(sel, ht, red, up, above, below, left, right):
+def blacken(sel, ht, red, up, border):
     vmem = pl.BlockSpec(memory_space=pltpu.VMEM)
     return pl.pallas_call(
         black_kernel,
         out_shape=jax.ShapeDtypeStruct((ROWS, COLS), f32),
-        in_specs=[vmem] * 8,
+        in_specs=[vmem] * 5,
         out_specs=vmem,
-        scratch_shapes=[pltpu.VMEM((COLS, ROWS), f32)],
-    )(sel, ht, red, up, above, below, left, right)
-
-
-def shifted(array, axis, step):
-    size = lax.axis_size(axis)
-    pairs = [(i, i + step) for i in range(size) if 0 <= i + step < size]
-    return lax.ppermute(array, axis, pairs)
-
-
-def interp_matrix(fine_pos, coarse_start, coarse_pixel_number, coarse_total):
-    numerator = 2 * fine_pos + 1 - UPS
-    lower = numerator // (2 * UPS)
-    fraction = (numerator - lower * 2 * UPS).astype(f32) / (2.0 * UPS)
-    low_index = jnp.clip(lower, 0, coarse_total - 1) - coarse_start
-    high_index = jnp.clip(lower + 1, 0, coarse_total - 1) - coarse_start
-    columns = jnp.arange(coarse_pixel_number, dtype=jnp.int32)
-    low_part = jnp.where(columns[None, :] == low_index[:, None], 1.0 - fraction[:, None], 0.0)
-    high_part = jnp.where(columns[None, :] == high_index[:, None], fraction[:, None], 0.0)
-    return low_part + high_part
-
-
-def jacobi_step(line_span, disp, conf):
-    col_pad = jnp.pad(line_span[1:-1], ((0, 0), (1, 1)))
-    neighbours = line_span[:-2] + line_span[2:] + col_pad[:, :-2] + col_pad[:, 2:]
-    return (conf * disp + neighbours) / (conf + 4.0)
-
-
-def upsample(coarse_disp, coarse_conf):
-    row_index = lax.axis_index("row")
-    col_index = lax.axis_index("col")
-    coarse_tile = ROWS // UPS
-    disp = lax.all_gather(coarse_disp, "col", axis=0, tiled=True)
-    conf = lax.all_gather(coarse_conf, "col", axis=0, tiled=True)
-    height, width = disp.shape
-    current = disp
-    for _ in range(CITER):
-        current = jacobi_step(jnp.pad(current, ((1, 1), (0, 0))), disp, conf)
-    spread = jnp.pad(current, ((1, 1), (0, 0)))
-    piece = lax.dynamic_slice_in_dim(spread, row_index * coarse_tile, coarse_tile + 2, 0)
-    row_mat = interp_matrix(row_index * ROWS + jnp.arange(ROWS, dtype=jnp.int32),
-                            row_index * coarse_tile - 1, coarse_tile + 2, height)
-    order = jnp.arange(COLS, dtype=jnp.int32)
-    order = (order % SEGS) * SEG + order // SEGS
-    col_mat = interp_matrix(col_index * COLS + order, 0, width, width)
-    high = lax.Precision.HIGHEST
-    return jnp.dot(col_mat, jnp.dot(row_mat, piece, precision=high).T, precision=high)
-
-
-def spread_tiles(reference_image, source_images):
-    stacked = jnp.concatenate([reference_image[None], source_images], 0)
-    above = shifted(stacked[:, ROWS - R:, :], "row", 1)
-    below = shifted(stacked[:, :R, :], "row", -1)
-    tall = jnp.concatenate([stacked, above, below], 1)
-    west = shifted(tall[:, :, COLS - LEFT:], "col", 1)
-    east = shifted(tall[:, :, :8], "col", -1)
-    wide = jnp.concatenate([west, tall, east], 2)
-    wide = jnp.pad(wide, ((0, 0), (0, 0), (PADL - LEFT, 0)))
-    turned = jnp.transpose(wide, (0, 2, 1))
-    main = turned[:, :, :ROWS]
-    edge = turned[:, :, ROWS:]
-    ref = jnp.concatenate([edge[0]] * SRC, 1)
-    src = jnp.concatenate([edge[v + 1] for v in range(SRC)], 1)
-    edges = jnp.pad(jnp.stack([ref, src]), ((0, 0), (0, 0), (0, 128 - SRC * HL)))
-    return main, edges
+        scratch_shapes=[
+            pltpu.VMEM((COLS, ROWS), f32),
+            pltpu.VMEM((4, 8, 128), f32),
+            pltpu.SemaphoreType.DMA((4,)),
+            pltpu.SemaphoreType.DMA((4,)),
+        ],
+        compiler_params=pltpu.CompilerParams(collective_id=1, has_side_effects=True),
+    )(sel, ht, red, up, border)
 
 
 def on_device(reference_image, source_images, hypotheses, source_ids, coarse_disp, coarse_conf):
-    up = upsample(coarse_disp, coarse_conf)
-    main, edges = spread_tiles(reference_image, source_images)
-    sel, ht, red = score(source_ids, main, edges, hypotheses, up)
-    border = border_lanes(red)
-    above = shifted(border, "row", 1)
-    below = shifted(border, "row", -1)
-    left = shifted(red[8 * SEG - 8:], "col", 1)
-    right = shifted(red[:8], "col", -1)
-    return blacken(sel, ht, red, up, above, below, left, right)
+    xm, href, hsrc, cb, ht = exchange(reference_image, source_images, hypotheses, coarse_disp, coarse_conf)
+    shape = (coarse_disp.shape[0] * lax.axis_size("col"), coarse_disp.shape[1])
+    sel, up, red, border = score(source_ids, xm, href, hsrc, cb, ht, shape)
+    return blacken(sel, ht, red, up, border)
 
 
 def solution(mesh):

time: 227 us -> 57.5 us (0.25)
  the two profiles are of different devices: /device:TPU:33 before, /device:TPU:95 now
where the time goes in v2:
time: 57.5 us; the launch traced here: 57.3 us
  Pallas kernels  55.7 us (97%)
  local copies, waits for them, and re-layouts  1.57 us (3%)
    pallas_call x1, Pallas kernels, score(): pl.pallas_call(functools.partial(score_kernel, coarse_shape), out_shape=(...  23 us
    pallas_call x1, Pallas kernels, exchange(): pl.pallas_call(exchange_kernel, out_shape=(jax.ShapeDtypeStruct((SRC + 1,...  18.7 us
    pallas_call x1, Pallas kernels, blacken(): pl.pallas_call(black_kernel, out_shape=jax.ShapeDtypeStruct((ROWS, COLS),...  14.1 us
    unnamed x1, local copies, waits for them, and re-layouts  1.57 us

profile of v2, /device:TPU:95, one launch (start us, length us, event | category | flops | bytes accessed | tf_op | source)
XLA Modules:
  0.0 57.3 jit_solution(2206067048393454779)
XLA Ops:
  0.0 18.7 %shard_map.64 = (f32[5,320,128]{2,1,0:T(8,128)}, f32[2,8,512]{2,1,0:T(8,128)}, f32[2,4,8,512]{3,2,1,0:T(8,128)}, f32[2,32,256]{2,1,0:T(8,128)}, s32[256,128]{1,0:T(8,128)}) custom-call(f32[128,256]{1,0:T(8,128)} %ref.1, f32[4,128,256]{2,1,0:T(8,128)} %src.1, s32[8,128,256]{2,1,0:T(8,128)} %hyp.1, f32[32,512]{1,0:T(8,128)} %disp.1, f32[32,512]{1,0:T(8,128)} %conf.1), custom_call_target="tpu_custom_call" | custom-call | tf_op jit(solution)/shard_map/pallas_call | solution.py:252
  18.7 23.0 %shard_map.65 = (f32[8,256,128]{2,1,0:T(8,128)}, f32[256,128]{1,0:T(8,128)}, f32[256,128]{1,0:T(8,128)}, f32[8,128]{1,0:T(8,128)}) custom-call(s32[4]{0:T(128)} %ids.1, f32[5,320,128]{2,1,0:T(8,128)} %get-tuple-element.14.xm, f32[2,8,512]{2,1,0:T(8,128)} %get-tuple-element.15.href, f32[2,4,8,512]{3,2,1,0:T(8,128)} %get-tuple-element.16.hsrc, ...), custom_call_target="tpu_custom_call" | custom-call | tf_op jit(solution)/shard_map/pallas_call | solution.py:462
  41.7 14.1 %shard_map.66 = f32[128,256]{1,0:T(8,128)} custom-call(f32[8,256,128]{2,1,0:T(8,128)} %get-tuple-element.19.sel, s32[256,128]{1,0:T(8,128)} %get-tuple-element.18.ht_ref.ht, f32[256,128]{1,0:T(8,128)} %get-tuple-element.20.red, f32[256,128]{1,0:T(8,128)} %get-tuple-element.21.up, f32[8,128]{1,0:T(8,128)} %get-tuple-element.22.border), custom_call_target="tpu_custom_call" | custom-call | tf_op jit(solution)/shard_map/pallas_call | solution.py:583
  55.8 1.6 %copy.8 = f32[128,256]{1,0:T(8,128)} copy(f32[128,256]{1,0:T(8,128)} %shard_map.66) | data formatting | bytes 262144

commit v3 on v1

v3 whole, which is shorter than its diff:
```python
import functools

import jax
import jax.numpy as jnp
from jax import lax
from jax.experimental import pallas as pl
from jax.experimental.pallas import tpu as pltpu
from jax.sharding import PartitionSpec as P

LEVELS = 16
HYP = 8
SRC = 4
MAXID = 3
WIN = 11
UPS = 8
CITER = 4
R = WIN // 2
AREA = float(WIN * WIN)
FLOOR = 1e-05

ROWS, COLS = 128, 256
SEGS = 8
SEG = COLS // SEGS
SHIFT = MAXID * (LEVELS - 1)
LEFT = SHIFT + R
PADL = 56
CI = 320
NJ = SEG + 2 * R + SHIFT
NK = SEG + 2 * R
NM = SEG + SHIFT
HL = 2 * R
bf16 = jnp.bfloat16
f32 = jnp.float32


def window11(vals):
    n = len(vals)
    count = n - WIN + 1
    suf, pre = {}, {}
    for start in range(0, n, WIN):
        stop = min(start + WIN, n)
        if stop - start == WIN and start < count:
            acc = vals[stop - 1]
            suf[stop - 1] = acc
            for i in range(stop - 2, start - 1, -1):
                acc = vals[i] + acc
                suf[i] = acc
        if start:
            acc = vals[start]
            pre[start] = acc
            for i in range(start + 1, min(stop, start + WIN - 1)):
                acc = acc + vals[i]
                pre[i] = acc
    return [suf[i] if i % WIN == 0 else suf[i] + pre[i + WIN - 1] for i in range(count)]


def parts(value, count):
    out = []
    for _ in range(count - 1):
        piece = value.astype(bf16)
        out.append(piece)
        value = value - piece.astype(f32)
    out.append(value.astype(bf16))
    return out


def put_parts(ref, sums, columns):
    n = len(sums)
    for q in range(0, n, 2):
        both = jnp.concatenate(sums[q:q + 2], axis=0) if q + 1 < n else sums[q]
        for piece, col in zip(parts(both, len(columns)), columns):
            ref[8 * q:8 * q + both.shape[0], col:col + 128] = piece


def band_main():
    a = lax.broadcasted_iota(jnp.int32, (ROWS, ROWS), 0)
    b = lax.broadcasted_iota(jnp.int32, (ROWS, ROWS), 1)
    return jnp.where(jnp.abs(a - b) <= R, 1.0, 0.0).astype(bf16)


def band_halo(view):
    a = lax.broadcasted_iota(jnp.int32, (128, ROWS), 0) - view * HL
    b = lax.broadcasted_iota(jnp.int32, (128, ROWS), 1)
    row = jnp.where(a < R, a - R, a - R + ROWS)
    good = (a >= 0) & (a < HL) & (jnp.abs(row - b) <= R)
    return jnp.where(good, 1.0, 0.0).astype(bf16)


def interp_block(fine, coarse_start, total, shape):
    numerator = 2 * fine + 1 - UPS
    lower = numerator >> 4
    fraction = (numerator - lower * 2 * UPS).astype(f32) / (2.0 * UPS)
    where = lax.broadcasted_iota(jnp.int32, shape, 1) + coarse_start
    low = jnp.where(where == jnp.clip(lower, 0, total - 1), 1.0 - fraction, 0.0)
    high = jnp.where(where == jnp.clip(lower + 1, 0, total - 1), fraction, 0.0)
    return low + high


def upsampled_tile(cb, total_rows, total_cols):
    row, col = lax.axis_index("row"), lax.axis_index("col")
    high, wide = cb.shape[1:]
    start = 16 * row - 8
    begin = 128 * jnp.clip((32 * col + 123) // 128 - 1, 0, (total_cols - wide) // 128)
    disp, conf = cb[0], cb[1]
    place = lax.broadcasted_iota(jnp.int32, (high, wide), 0) + start
    lane = lax.broadcasted_iota(jnp.int32, (high, wide), 1)
    good = (place >= 0) & (place < total_rows)
    local = lax.broadcasted_iota(jnp.int32, (high, wide), 0)
    pull = conf * disp
    current = disp
    for _ in range(CITER):
        up = jnp.where(local == 0, 0.0, pltpu.roll(current, 1, 0))
        down = jnp.where(local == high - 1, 0.0, pltpu.roll(current, high - 1, 0))
        left = jnp.where(lane == 0, 0.0, pltpu.roll(current, 1, 1))
        right = jnp.where(lane == wide - 1, 0.0, pltpu.roll(current, wide - 1, 1))
        current = jnp.where(good, (pull + (up + down + left + right)) / (conf + 4.0), 0.0)
    fine_rows = row * ROWS + lax.broadcasted_iota(jnp.int32, (ROWS, high), 0)
    order = lax.broadcasted_iota(jnp.int32, (COLS, wide), 0)
    fine_cols = col * COLS + (order & (SEGS - 1)) * SEG + (order >> 3)
    row_mat = interp_block(fine_rows, start, total_rows, (ROWS, high))
    col_mat = interp_block(fine_cols, begin, total_cols, (COLS, wide))
    best = lax.Precision.HIGHEST
    tall = jnp.dot(row_mat, current, precision=best, preferred_element_type=f32)
    return lax.dot_general(col_mat, tall, (((1,), (1,)), ((), ())), precision=best, preferred_element_type=f32)


MESH = pl.DeviceIdType.MESH


def stereo_kernel(coarse_shape, ids, ref_in, src_in, hyp_in, disp_in, conf_in, out,
                  img, hyp, coarse, xm, hal, cb, ht, htc, sel, up, red, border, tmp, near,
                  xs, hs, rt, rx3, rmom, xmom, lmom, cmom, av, bv, lhs, lx, yy, vol, zt,
                  load, local, send, recv, csend, crecv):
    row, col = lax.axis_index("row"), lax.axis_index("col")
    nr, nc = lax.axis_size("row"), lax.axis_size("col")
    wide = cb.shape[2]
    last = (coarse_shape[1] - wide) // 128

    loads = [
        pltpu.make_async_copy(ref_in, img.at[0], load.at[0]),
        pltpu.make_async_copy(src_in, img.at[pl.ds(1, SRC)], load.at[1]),
        pltpu.make_async_copy(disp_in, coarse.at[0], load.at[2]),
        pltpu.make_async_copy(conf_in, coarse.at[1], load.at[3]),
        pltpu.make_async_copy(hyp_in, hyp, load.at[4]),
    ]
    for copy in loads:
        copy.start()

    def inside(dr, dc):
        good = row >= 0
        if dr:
            good = good & ((row > 0) if dr < 0 else (row < nr - 1))
        if dc:
            good = good & ((col > 0) if dc < 0 else (col < nc - 1))
        return good

    def away(dr, dc):
        return {"row": lax.rem(row + dr + nr, nr), "col": lax.rem(col + dc + nc, nc)}

    around = [(dr, dc) for dr in (-1, 0, 1) for dc in (-1, 0, 1) if dr or dc]
    odd = lax.rem(row, 2)
    main_col = row // 2
    side_col = main_col - 1 + 2 * odd
    side_there = (side_col >= 0) & (side_col < nc)
    is_main = col == main_col
    is_side = col == side_col

    barrier = pltpu.get_barrier_semaphore()
    expected = jnp.int32(0)
    for dr, dc in around:
        expected += inside(dr, dc).astype(jnp.int32)

        @pl.when(inside(dr, dc))
        def _(dr=dr, dc=dc):
            pl.semaphore_signal(barrier, inc=1, device_id=away(dr, dc), device_id_type=MESH)

    @pl.when(jnp.logical_not(is_main))
    def _():
        pl.semaphore_signal(barrier, inc=1, device_id={"row": row, "col": main_col}, device_id_type=MESH)

    @pl.when(side_there & jnp.logical_not(is_side))
    def _():
        pl.semaphore_signal(barrier, inc=1, device_id={"row": row, "col": jnp.clip(side_col, 0, nc - 1)}, device_id_type=MESH)

    expected += (nc - 1) * (is_main.astype(jnp.int32) + is_side.astype(jnp.int32))
    pl.semaphore_wait(barrier, expected)

    copies = []

    def push(dr, dc, source, target):
        n = len(copies)
        copy = pltpu.make_async_remote_copy(source, target, send.at[n], recv.at[n], device_id=away(dr, dc), device_id_type=MESH)
        copies.append((dr, dc, copy, target))

        @pl.when(inside(dr, dc))
        def _():
            copy.start()

    def arrive(entries):
        for dr, dc, copy, target in entries:
            @pl.when(inside(-dr, -dc))
            def _(copy=copy):
                copy.wait_recv()

            @pl.when(jnp.logical_not(inside(-dr, -dc)))
            def _(target=target):
                target[...] = jnp.zeros(target.shape, f32)

    def leave(entries):
        for dr, dc, copy, target in entries:
            @pl.when(inside(dr, dc))
            def _(copy=copy):
                copy.wait_send()

    loads[0].wait()
    loads[1].wait()
    for dc in (1, -1, 0):
        lanes = {0: (0, COLS), 1: (COLS - 128, 128), -1: (0, 128)}[dc]
        to = {0: 128, 1: 0, -1: 384}[dc]
        for dr in (1, -1):
            here = pl.ds(ROWS - 8, 8) if dr == 1 else pl.ds(0, 8)
            side = 0 if dr == 1 else 1
            push(dr, dc, img.at[:, here, pl.ds(*lanes)], hal.at[side, :, :, pl.ds(to, lanes[1])])

    for v in range(SRC + 1):
        xm[v, PADL:PADL + COLS, :] = img[v].T
    push(0, 1, xm.at[pl.ds(1, SRC), pl.ds(COLS, PADL), :], xm.at[pl.ds(1, SRC), pl.ds(0, PADL), :])
    push(0, -1, xm.at[:, pl.ds(PADL, 8), :], xm.at[:, pl.ds(PADL + COLS, 8), :])
    push(0, 1, xm.at[pl.ds(0, 1), pl.ds(PADL + COLS - 8, 8), :], xm.at[pl.ds(0, 1), pl.ds(PADL - 8, 8), :])
    halos = list(copies)

    loads[2].wait()
    loads[3].wait()
    main_src = pl.ds(pl.multiple_of(8 * odd, 8), 24)
    main_dst = cb.at[:, pl.ds(pl.multiple_of(8 - 8 * odd, 8), 24), :]
    side_src = pl.ds(pl.multiple_of(24 - 24 * odd, 8), 8)
    side_dst = cb.at[:, pl.ds(pl.multiple_of(24 * odd, 8), 8), :]

    def coarse_copy(j, rows, target, kind):
        lanes = pl.ds(pl.multiple_of(128 * jnp.clip((32 * j + 123) // 128 - 1, 0, last), 128), wide)
        source = coarse.at[:, rows, lanes]
        return pltpu.make_async_remote_copy(source, target, csend.at[j], crecv.at[kind], device_id={"row": row, "col": j}, device_id_type=MESH)

    def coarse_own(rows, target):
        lanes = pl.ds(pl.multiple_of(128 * jnp.clip((32 * col + 123) // 128 - 1, 0, last), 128), wide)
        return pltpu.make_async_copy(coarse.at[:, rows, lanes], target, local.at[0])

    kinds = ((is_main, main_src, main_dst, 0), (is_side, side_src, side_dst, 1))
    for role, rows, target, kind in kinds:
        @pl.when(role)
        def _(rows=rows, target=target, kind=kind):
            def one(j, carry):
                @pl.when(j != col)
                def _():
                    coarse_copy(j, rows, target, kind).start()

                return carry

            lax.fori_loop(0, nc, one, 0)
            coarse_own(rows, target).start()

    loads[4].wait()
    packed = hyp[0]
    for k in range(1, HYP):
        packed = packed | (hyp[k] << (4 * k))
    htc[...] = packed.T
    for i in range(SEG):
        ht[8 * i:8 * i + 8, :] = htc[pl.ds(i, SEGS, stride=SEG), :]

    zero = jnp.zeros((128, 128), bf16)
    b = band_main()
    halo = [band_halo(v) for v in range(SRC)]
    rt[0:128, 0:128] = b
    rt[0:128, 128:256] = zero
    rt[128:256, 0:128] = zero
    rt[128:256, 128:256] = b
    for v in range(SRC):
        rmom[v, 0:128, 0:128] = halo[v]
        rmom[v, 0:128, 128:256] = zero
        rmom[v, 128:256, 0:128] = zero
        rmom[v, 128:256, 128:256] = halo[v]
        p, q = v // 2, v % 2
        rx3[p, 0:128, 128 * q:128 * q + 128] = halo[v]
        rx3[p, 128:256, 128 * q:128 * q + 128] = halo[v]


    arrive(halos)
    gap = jnp.zeros((64 - SRC * HL, 512), f32)
    stack = []
    for v in range(SRC):
        stack += [hal[0, v + 1, 8 - R:8, :], hal[1, v + 1, 0:R, :]]
    stack.append(gap)
    for v in range(SRC):
        stack += [hal[0, 0, 8 - R:8, :], hal[1, 0, 0:R, :]]
    stack.append(gap)
    zt[...] = jnp.concatenate(stack, axis=0).T
    for j in range(NJ):
        rows = pl.ds(j + PADL - LEFT, SEGS, stride=SEG)
        for v in range(SRC):
            xs[v + 1, j] = xm[v + 1, rows, :]
        edge = zt[pl.ds(j + 128 - LEFT, SEGS, stride=SEG), :]
        hs[1, j] = edge
        if j >= SHIFT:
            xs[0, j] = xm[0, rows, :]
            hs[0, j] = pltpu.roll(edge, 64, 1)

    def moments(load, first, count, ref):
        vals = [load(first + j) for j in range(count)]
        put_parts(ref, window11(vals), (0, 256, 512))
        vals = [load(first + j) for j in range(count)]
        put_parts(ref, window11([x * x for x in vals]), (128, 384, 640))

    def finish(rows, view):
        total = jnp.dot(lmom[0:rows, 0:256], rt[...], preferred_element_type=f32)
        for t in (256, 512):
            total += jnp.dot(lmom[0:rows, t:t + 256], rt[...], preferred_element_type=f32)
        for t in (0, 256, 512):
            total += jnp.dot(xmom[0:rows, t:t + 256], rmom[view], preferred_element_type=f32)
        cmom[0:rows, :] = total

    moments(lambda j: hs[0, j], SHIFT, NK, xmom)
    moments(lambda j: xs[0, j], SHIFT, NK, lmom)
    finish(SEG * 8, 0)
    for i in range(SEG):
        m = cmom[8 * i:8 * i + 8, 0:128] / AREA
        var = cmom[8 * i:8 * i + 8, 128:256] / AREA - m * m + FLOOR
        av[0, i] = lax.rsqrt(var)
        bv[0, i] = m

    moments(lambda j: hs[1, j], 0, NJ, xmom)

    def view_moments(v, carry):
        moments(lambda j: xs[v + 1, j], 0, NJ, lmom)
        finish(NM * 8, v)

        def fill(i, c):
            rows = pl.ds(pl.multiple_of(8 * i, 8), 8)
            m = cmom[rows, 0:128] / AREA
            var = cmom[rows, 128:256] / AREA - m * m + FLOOR
            inv = lax.rsqrt(var) / SRC
            av[v + 1, i] = inv / AREA
            bv[v + 1, i] = m * inv
            return c

        return lax.fori_loop(0, NM, fill, carry)

    lax.fori_loop(0, SRC, view_moments, 0)

    lane = lax.broadcasted_iota(jnp.int32, (8, 128), 1)
    masks = [lane < HL * (v + 1) for v in range(SRC - 1)]

    def level(l, carry):
        begins = [SHIFT - ids[v] * l for v in range(SRC)]
        prods = []
        for k in range(NK):
            piece = hs[1, begins[3] + k]
            for v in (2, 1, 0):
                piece = jnp.where(masks[v], hs[1, begins[v] + k], piece)
            prods.append(hs[0, SHIFT + k] * piece)
        put_parts(lx, window11(prods), (0, 128))
        for v in range(SRC):
            prods = [xs[0, SHIFT + k] * xs[v + 1, begins[v] + k] for k in range(NK)]
            put_parts(lhs.at[v // 2], window11(prods), (128 * (v % 2), 256 + 128 * (v % 2)))
        for p in range(SRC // 2):
            total = jnp.dot(lhs[p, :, 0:256], rt[...], preferred_element_type=f32)
            total += jnp.dot(lhs[p, :, 256:512], rt[...], preferred_element_type=f32)
            total += jnp.dot(lx[...], rx3[p], preferred_element_type=f32)
            yy[p] = total
        for i in range(SEG):
            rows = slice(8 * i, 8 * i + 8)
            acc = None
            sub = None
            for v in range(SRC):
                y = yy[v // 2, rows, 128 * (v % 2):128 * (v % 2) + 128]
                a = y * av[v + 1, begins[v] + i]
                s = bv[v + 1, begins[v] + i]
                acc = a if acc is None else acc + a
                sub = s if sub is None else sub + s
            vol[l, i] = av[0, i] * (acc - bv[0, i] * sub)
        return carry

    lax.fori_loop(0, LEVELS, level, 0)

    for role, rows, target, kind in kinds:
        there = side_there if kind else col >= 0

        @pl.when(role)
        def _(rows=rows, target=target, kind=kind):
            coarse_own(rows, target).wait()

        @pl.when(jnp.logical_not(role) & there)
        def _(rows=rows, target=target, kind=kind):
            coarse_copy(col, rows, target, kind).wait_recv()

    @pl.when(jnp.logical_not(side_there))
    def _():
        side_dst[...] = jnp.zeros(side_dst.shape, f32)

    up[...] = upsampled_tile(cb, *coarse_shape)

    def pick(i, carry):
        rows = pl.ds(pl.multiple_of(8 * i, 8), 8)
        codes = ht[rows, :]
        centre = up[rows, :]
        num = jnp.zeros((8, 128), f32)
        den = jnp.zeros((8, 128), f32)
        for k in range(HYP):
            table = [vol[l, i] for l in range(LEVELS)]
            for bit in range(4):
                odd = (codes & jnp.int32((1 << (4 * k + bit)) - (1 << 32 if 4 * k + bit == 31 else 0))) != 0
                table = [jnp.where(odd, table[t + 1], table[t]) for t in range(0, len(table), 2)]
            gain = 10.0 * table[0] - 10.0
            sel[k, rows, :] = gain
            cand = (lax.shift_right_logical(codes, 4 * k) & 15).astype(f32)
            d = cand - centre
            w = jnp.exp(gain - 0.1 * (d * d))
            num += w * cand
            den += w
        red[rows, :] = num / den
        return carry

    lax.fori_loop(0, SEG, pick, 0)


    lane = lax.broadcasted_iota(jnp.int32, (8, 128), 1)
    edge = jnp.zeros((8, 128), f32)
    for i in range(SEG):
        v = red[8 * i:8 * i + 8, :]
        edge = jnp.where(lane == i, jnp.broadcast_to(v[:, 0:1], (8, 128)), edge)
        edge = jnp.where(lane == SEG + i, jnp.broadcast_to(v[:, 127:128], (8, 128)), edge)
    border[...] = edge


    copies.clear()
    copies.extend(halos)
    push(0, 1, red.at[pl.ds(8 * SEG - 8, 8), :], near.at[2])
    push(0, -1, red.at[pl.ds(0, 8), :], near.at[3])
    push(1, 0, border, near.at[0])
    push(-1, 0, border, near.at[1])
    final = copies[len(halos):]

    leave(halos)
    for role, rows, target, kind in kinds:
        @pl.when(role)
        def _(rows=rows, target=target, kind=kind):
            def one(j, carry):
                @pl.when(j != col)
                def _():
                    coarse_copy(j, rows, target, kind).wait_send()

                return carry

            lax.fori_loop(0, nc, one, 0)

    arrive(final)
    lane = lax.broadcasted_iota(jnp.int32, (8, 128), 1)
    seg = lax.broadcasted_iota(jnp.int32, (8, 128), 0)
    row_edge = jnp.where((lane == 0) & (row == 0), 1.0, 0.0) + jnp.where(
        (lane == ROWS - 1) & (row == nr - 1), 1.0, 0.0)
    above_v = near[0]
    below_v = near[1]
    left, right = near.at[2], near.at[3]
    for i in range(SEG):
        rows = slice(8 * i, 8 * i + 8)
        r = red[rows, :]
        u = up[rows, :]
        h = ht[rows, :]
        north = jnp.where(lane == 0, jnp.broadcast_to(above_v[:, SEG + i:SEG + i + 1], (8, 128)), pltpu.roll(r, 1, 1))
        south = jnp.where(lane == ROWS - 1, jnp.broadcast_to(below_v[:, i:i + 1], (8, 128)), pltpu.roll(r, ROWS - 1, 1))
        if i == 0:
            west = jnp.concatenate([left[7:8, :], red[8 * SEG - 8:8 * SEG - 1, :]], axis=0)
        else:
            west = red[8 * i - 8:8 * i, :]
        if i == SEG - 1:
            east = jnp.concatenate([red[1:8, :], right[0:1, :]], axis=0)
        else:
            east = red[8 * i + 8:8 * i + 16, :]
        count = 4.0 - row_edge
        if i == 0:
            count = count - jnp.where((seg == 0) & (col == 0), 1.0, 0.0)
        if i == SEG - 1:
            count = count - jnp.where((seg == 7) & (col == nc - 1), 1.0, 0.0)
        centre = 0.5 * u + 0.5 * (north + south + west + east) / count
        num = jnp.zeros((8, 128), f32)
        den = jnp.zeros((8, 128), f32)
        for k in range(HYP):
            cand = (lax.shift_right_logical(h, 4 * k) & 15).astype(f32)
            d = cand - centre
            w = jnp.exp(sel[k, rows, :] - 0.1 * (d * d))
            num += w * cand
            den += w
        even = ((lane + i) & 1) == 0
        tmp[pl.ds(i, SEGS, stride=SEG), :] = jnp.where(even, r, num / den)
    out[...] = tmp[...].T
    leave(final)


def on_device(reference_image, source_images, hypotheses, source_ids, coarse_disp, coarse_conf):
    shape = (coarse_disp.shape[0] * lax.axis_size("col"), coarse_disp.shape[1])
    anywhere = pl.BlockSpec(memory_space=pl.ANY)
    n = SEG * 8
    return pl.pallas_call(
        functools.partial(stereo_kernel, shape),
        out_shape=jax.ShapeDtypeStruct((ROWS, COLS), f32),
        in_specs=[pl.BlockSpec(memory_space=pltpu.SMEM)] + [anywhere] * 5,
        out_specs=pl.BlockSpec(memory_space=pltpu.VMEM),
        scratch_shapes=[
            pltpu.VMEM((SRC + 1, ROWS, COLS), f32),
            pltpu.VMEM((HYP, ROWS, COLS), jnp.int32),
            pltpu.VMEM((2,) + coarse_disp.shape, f32),
            pltpu.VMEM((SRC + 1, CI, 128), f32),
            pltpu.VMEM((2, SRC + 1, 8, 512), f32),
            pltpu.VMEM((2, 32, min(256, coarse_disp.shape[1])), f32),
            pltpu.VMEM((n, 128), jnp.int32),
            pltpu.VMEM((COLS, ROWS), jnp.int32),
            pltpu.VMEM((HYP, n, 128), f32),
            pltpu.VMEM((n, 128), f32),
            pltpu.VMEM((n, 128), f32),
            pltpu.VMEM((8, 128), f32),
            pltpu.VMEM((COLS, ROWS), f32),
            pltpu.VMEM((4, 8, 128), f32),
            pltpu.VMEM((SRC + 1, NJ, 8, 128), f32),
            pltpu.VMEM((2, NJ, 8, 128), f32),
            pltpu.VMEM((256, 256), bf16),
            pltpu.VMEM((2, 256, 256), bf16),
            pltpu.VMEM((SRC, 256, 256), bf16),
            pltpu.VMEM((NM * 8 + 8, 768), bf16),
            pltpu.VMEM((NM * 8 + 8, 768), bf16),
            pltpu.VMEM((NM * 8, 256), f32),
            pltpu.VMEM((SRC + 1, NM, 8, 128), f32),
            pltpu.VMEM((SRC + 1, NM, 8, 128), f32),
            pltpu.VMEM((2, n, 512), bf16),
            pltpu.VMEM((n, 256), bf16),
            pltpu.VMEM((2, n, 256), f32),
            pltpu.VMEM((LEVELS, SEG, 8, 128), f32),
            pltpu.VMEM((512, 128), f32),
            pltpu.SemaphoreType.DMA((5,)),
            pltpu.SemaphoreType.DMA((1,)),
            pltpu.SemaphoreType.DMA((13,)),
            pltpu.SemaphoreType.DMA((13,)),
            pltpu.SemaphoreType.DMA((16,)),
            pltpu.SemaphoreType.DMA((2,)),
        ],
        compiler_params=pltpu.CompilerParams(collective_id=0, has_side_effects=True),
    )(source_ids, reference_image, source_images, hypotheses, coarse_disp, coarse_conf)


def solution(mesh):
    in_specs = (
        P("row", "col"),
        P(None, "row", "col"),
        P(None, "row", "col"),
        P(),
        P("col", None),
        P("col", None),
    )
    return jax.shard_map(
        on_device, mesh=mesh, in_specs=in_specs, out_specs=P("row", "col"), check_vma=False
    )
```

time: 227 us -> 42.4 us (0.19)
  the two profiles are of different devices: /device:TPU:33 before, /device:TPU:9 now
where the time goes in v3:
time: 42.4 us; the launch traced here: 42.3 us
  Pallas kernels  40.7 us (96%)
  local copies, waits for them, and re-layouts  1.57 us (4%)
    pallas_call x1, Pallas kernels, on_device(): pl.pallas_call(functools.partial(stereo_kernel, shape), out_shape=jax.Sha...  40.7 us
    unnamed x1, local copies, waits for them, and re-layouts  1.57 us

profile of v3, /device:TPU:9, one launch (start us, length us, event | category | flops | bytes accessed | tf_op | source)
XLA Modules:
  0.0 42.3 jit_solution(10660909845744640752)
XLA Ops:
  0.0 40.7 %shard_map.64 = f32[128,256]{1,0:T(8,128)} custom-call(s32[4]{0:T(128)} %ids.1, f32[128,256]{1,0:T(8,128)} %ref_in.1, f32[4,128,256]{2,1,0:T(8,128)} %src_in.1, s32[8,128,256]{2,1,0:T(8,128)} %hyp_in.1, f32[32,512]{1,0:T(8,128)} %disp_in.1, f32[32,512]{1,0:T(8,128)} %conf_in.1), custom_call_target="tpu_custom_call" | custom-call | tf_op jit(solution)/shard_map/pallas_call | solution.py:502
  40.7 1.6 %copy.8 = f32[128,256]{1,0:T(8,128)} copy(f32[128,256]{1,0:T(8,128)} %shard_map.64) | data formatting | bytes 262144

commit v4 on v3

--- a/solution.py
+++ b/solution.py
@@ -29,6 +29,8 @@
 NK = SEG + 2 * R
 NM = SEG + SHIFT
 HL = 2 * R
+LB = 2
+VMEM_LIMIT = 60 * 1024 * 1024
 bf16 = jnp.bfloat16
 f32 = jnp.float32
 
@@ -96,11 +98,25 @@
     return low + high
 
 
-def upsampled_tile(cb, total_rows, total_cols):
+def coarse_window(total_cols, wide):
     row, col = lax.axis_index("row"), lax.axis_index("col")
+    return 16 * row - 8, 128 * jnp.clip((32 * col + 123) // 128 - 1, 0, (total_cols - wide) // 128)
+
+
+def interp_mats(row_mat, col_mat, total_rows, total_cols):
+    row, col = lax.axis_index("row"), lax.axis_index("col")
+    high, wide = row_mat.shape[1], col_mat.shape[1]
+    start, begin = coarse_window(total_cols, wide)
+    fine_rows = row * ROWS + lax.broadcasted_iota(jnp.int32, (ROWS, high), 0)
+    order = lax.broadcasted_iota(jnp.int32, (COLS, wide), 0)
+    fine_cols = col * COLS + (order & (SEGS - 1)) * SEG + (order >> 3)
+    row_mat[...] = interp_block(fine_rows, start, total_rows, (ROWS, high)).astype(bf16)
+    col_mat[...] = interp_block(fine_cols, begin, total_cols, (COLS, wide)).astype(bf16)
+
+
+def upsampled_tile(cb, row_mat, col_mat, total_rows, total_cols):
     high, wide = cb.shape[1:]
-    start = 16 * row - 8
-    begin = 128 * jnp.clip((32 * col + 123) // 128 - 1, 0, (total_cols - wide) // 128)
+    start, _ = coarse_window(total_cols, wide)
     disp, conf = cb[0], cb[1]
     place = lax.broadcasted_iota(jnp.int32, (high, wide), 0) + start
     lane = lax.broadcasted_iota(jnp.int32, (high, wide), 1)
@@ -114,14 +130,13 @@
         left = jnp.where(lane == 0, 0.0, pltpu.roll(current, 1, 1))
         right = jnp.where(lane == wide - 1, 0.0, pltpu.roll(current, wide - 1, 1))
         current = jnp.where(good, (pull + (up + down + left + right)) / (conf + 4.0), 0.0)
-    fine_rows = row * ROWS + lax.broadcasted_iota(jnp.int32, (ROWS, high), 0)
-    order = lax.broadcasted_iota(jnp.int32, (COLS, wide), 0)
-    fine_cols = col * COLS + (order & (SEGS - 1)) * SEG + (order >> 3)
-    row_mat = interp_block(fine_rows, start, total_rows, (ROWS, high))
-    col_mat = interp_block(fine_cols, begin, total_cols, (COLS, wide))
-    best = lax.Precision.HIGHEST
-    tall = jnp.dot(row_mat, current, precision=best, preferred_element_type=f32)
-    return lax.dot_general(col_mat, tall, (((1,), (1,)), ((), ())), precision=best, preferred_element_type=f32)
+    tall = jnp.zeros((ROWS, wide), f32)
+    for piece in parts(current, 3):
+        tall += jnp.dot(row_mat[...], piece, preferred_element_type=f32)
+    out = jnp.zeros((COLS, ROWS), f32)
+    for piece in parts(tall, 3):
+        out += lax.dot_general(col_mat[...], piece, (((1,), (1,)), ((), ())), preferred_element_type=f32)
+    return out
 
 
 MESH = pl.DeviceIdType.MESH
@@ -129,7 +144,7 @@
 
 def stereo_kernel(coarse_shape, ids, ref_in, src_in, hyp_in, disp_in, conf_in, out,
                   img, hyp, coarse, xm, hal, cb, ht, htc, sel, up, red, border, tmp, near,
-                  xs, hs, rt, rx3, rmom, xmom, lmom, cmom, av, bv, lhs, lx, yy, vol, zt,
+                  xs, hs, rt, rx3, rmom, xmom, lmom, cmom, av, bv, lhs, lx, yy, vol, zt, row_mat, col_mat,
                   load, local, send, recv, csend, crecv):
     row, col = lax.axis_index("row"), lax.axis_index("col")
     nr, nc = lax.axis_size("row"), lax.axis_size("col")
@@ -183,8 +198,6 @@
         pl.semaphore_signal(barrier, inc=1, device_id={"row": row, "col": jnp.clip(side_col, 0, nc - 1)}, device_id_type=MESH)
 
     expected += (nc - 1) * (is_main.astype(jnp.int32) + is_side.astype(jnp.int32))
-    pl.semaphore_wait(barrier, expected)
-
     copies = []
 
     def push(dr, dc, source, target):
@@ -214,6 +227,9 @@
 
     loads[0].wait()
     loads[1].wait()
+    for v in range(SRC + 1):
+        xm[v, PADL:PADL + COLS, :] = img[v].T
+    pl.semaphore_wait(barrier, expected)
     for dc in (1, -1, 0):
         lanes = {0: (0, COLS), 1: (COLS - 128, 128), -1: (0, 128)}[dc]
         to = {0: 128, 1: 0, -1: 384}[dc]
@@ -222,8 +238,6 @@
             side = 0 if dr == 1 else 1
             push(dr, dc, img.at[:, here, pl.ds(*lanes)], hal.at[side, :, :, pl.ds(to, lanes[1])])
 
-    for v in range(SRC + 1):
-        xm[v, PADL:PADL + COLS, :] = img[v].T
     push(0, 1, xm.at[pl.ds(1, SRC), pl.ds(COLS, PADL), :], xm.at[pl.ds(1, SRC), pl.ds(0, PADL), :])
     push(0, -1, xm.at[:, pl.ds(PADL, 8), :], xm.at[:, pl.ds(PADL + COLS, 8), :])
     push(0, 1, xm.at[pl.ds(0, 1), pl.ds(PADL + COLS - 8, 8), :], xm.at[pl.ds(0, 1), pl.ds(PADL - 8, 8), :])
@@ -245,21 +259,8 @@
         lanes = pl.ds(pl.multiple_of(128 * jnp.clip((32 * col + 123) // 128 - 1, 0, last), 128), wide)
         return pltpu.make_async_copy(coarse.at[:, rows, lanes], target, local.at[0])
 
-    kinds = ((is_main, main_src, main_dst, 0), (is_side, side_src, side_dst, 1))
-    for role, rows, target, kind in kinds:
-        @pl.when(role)
-        def _(rows=rows, target=target, kind=kind):
-            def one(j, carry):
-                @pl.when(j != col)
-                def _():
-                    coarse_copy(j, rows, target, kind).start()
-
-                return carry
-
-            lax.fori_loop(0, nc, one, 0)
-            coarse_own(rows, target).start()
-
     loads[4].wait()
+    interp_mats(row_mat, col_mat, *coarse_shape)
     packed = hyp[0]
     for k in range(1, HYP):
         packed = packed | (hyp[k] << (4 * k))
@@ -284,7 +285,29 @@
         rx3[p, 128:256, 128 * q:128 * q + 128] = halo[v]
 
 
+    for j in range(NJ):
+        for v in range(SRC + 1):
+            if v or j >= SHIFT:
+                lo = 2 if j < LEFT - SEG else 1 if j < LEFT else 0
+                hi = SEGS - 1 if j >= NJ - R else SEGS
+                at = lo * SEG + j + PADL - LEFT
+                xs[v, j, lo:hi, :] = xm[v, pl.ds(at, hi - lo, stride=SEG), :]
+
     arrive(halos)
+    kinds = ((is_main, main_src, main_dst, 0), (is_side, side_src, side_dst, 1))
+    for role, rows, target, kind in kinds:
+        @pl.when(role)
+        def _(rows=rows, target=target, kind=kind):
+            def one(j, carry):
+                @pl.when(j != col)
+                def _():
+                    coarse_copy(j, rows, target, kind).start()
+
+                return carry
+
+            lax.fori_loop(0, nc, one, 0)
+            coarse_own(rows, target).start()
+
     gap = jnp.zeros((64 - SRC * HL, 512), f32)
     stack = []
     for v in range(SRC):
@@ -295,13 +318,21 @@
     stack.append(gap)
     zt[...] = jnp.concatenate(stack, axis=0).T
     for j in range(NJ):
-        rows = pl.ds(j + PADL - LEFT, SEGS, stride=SEG)
-        for v in range(SRC):
-            xs[v + 1, j] = xm[v + 1, rows, :]
+        if j < LEFT:
+            for v in range(SRC):
+                xs[v + 1, j, 0:1, :] = xm[v + 1, j + PADL - LEFT:j + PADL - LEFT + 1, :]
+                if j < LEFT - SEG:
+                    at = SEG + j + PADL - LEFT
+                    xs[v + 1, j, 1:2, :] = xm[v + 1, at:at + 1, :]
+        if SHIFT <= j < LEFT:
+            xs[0, j, 0:1, :] = xm[0, j + PADL - LEFT:j + PADL - LEFT + 1, :]
+        if j >= NJ - R:
+            at = (SEGS - 1) * SEG + j + PADL - LEFT
+            for v in range(SRC + 1):
+                xs[v, j, SEGS - 1:SEGS, :] = xm[v, at:at + 1, :]
         edge = zt[pl.ds(j + 128 - LEFT, SEGS, stride=SEG), :]
         hs[1, j] = edge
         if j >= SHIFT:
-            xs[0, j] = xm[0, rows, :]
             hs[0, j] = pltpu.roll(edge, 64, 1)
 
     def moments(load, first, count, ref):
@@ -333,53 +364,62 @@
         moments(lambda j: xs[v + 1, j], 0, NJ, lmom)
         finish(NM * 8, v)
 
-        def fill(i, c):
-            rows = pl.ds(pl.multiple_of(8 * i, 8), 8)
+        for i in range(NM):
+            rows = slice(8 * i, 8 * i + 8)
             m = cmom[rows, 0:128] / AREA
             var = cmom[rows, 128:256] / AREA - m * m + FLOOR
             inv = lax.rsqrt(var) / SRC
             av[v + 1, i] = inv / AREA
             bv[v + 1, i] = m * inv
-            return c
-
-        return lax.fori_loop(0, NM, fill, carry)
+        return carry
 
     lax.fori_loop(0, SRC, view_moments, 0)
 
     lane = lax.broadcasted_iota(jnp.int32, (8, 128), 1)
     masks = [lane < HL * (v + 1) for v in range(SRC - 1)]
 
-    def level(l, carry):
-        begins = [SHIFT - ids[v] * l for v in range(SRC)]
-        prods = []
-        for k in range(NK):
-            piece = hs[1, begins[3] + k]
-            for v in (2, 1, 0):
-                piece = jnp.where(masks[v], hs[1, begins[v] + k], piece)
-            prods.append(hs[0, SHIFT + k] * piece)
-        put_parts(lx, window11(prods), (0, 128))
-        for v in range(SRC):
-            prods = [xs[0, SHIFT + k] * xs[v + 1, begins[v] + k] for k in range(NK)]
-            put_parts(lhs.at[v // 2], window11(prods), (128 * (v % 2), 256 + 128 * (v % 2)))
+    def level(step, carry):
+        starts = []
+        for u in range(LB):
+            l = LB * step + u
+            begins = [SHIFT - ids[v] * l for v in range(SRC)]
+            starts.append((l, begins))
+            pieces = [hs[1, pl.ds(begins[v], NK)] for v in range(SRC)]
+            prods = []
+            for k in range(NK):
+                piece = pieces[3][k]
+                for v in (2, 1, 0):
+                    piece = jnp.where(masks[v], pieces[v][k], piece)
+                prods.append(hs[0, SHIFT + k] * piece)
+            part = pl.ds(256 * u, 256)
+            put_parts(lx.at[part], window11(prods), (0, 128))
+            for v in range(SRC):
+                moved = xs[v + 1, pl.ds(begins[v], NK)]
+                prods = [xs[0, SHIFT + k] * moved[k] for k in range(NK)]
+                put_parts(lhs.at[v // 2, part], window11(prods), (128 * (v % 2), 256 + 128 * (v % 2)))
         for p in range(SRC // 2):
             total = jnp.dot(lhs[p, :, 0:256], rt[...], preferred_element_type=f32)
             total += jnp.dot(lhs[p, :, 256:512], rt[...], preferred_element_type=f32)
             total += jnp.dot(lx[...], rx3[p], preferred_element_type=f32)
             yy[p] = total
-        for i in range(SEG):
-            rows = slice(8 * i, 8 * i + 8)
-            acc = None
-            sub = None
-            for v in range(SRC):
-                y = yy[v // 2, rows, 128 * (v % 2):128 * (v % 2) + 128]
-                a = y * av[v + 1, begins[v] + i]
-                s = bv[v + 1, begins[v] + i]
-                acc = a if acc is None else acc + a
-                sub = s if sub is None else sub + s
-            vol[l, i] = av[0, i] * (acc - bv[0, i] * sub)
+        for u in range(LB):
+            l, begins = starts[u]
+            scale = [av[v + 1, pl.ds(begins[v], SEG)] for v in range(SRC)]
+            shift = [bv[v + 1, pl.ds(begins[v], SEG)] for v in range(SRC)]
+            for i in range(SEG):
+                rows = slice(256 * u + 8 * i, 256 * u + 8 * i + 8)
+                acc = None
+                sub = None
+                for v in range(SRC):
+                    y = yy[v // 2, rows, 128 * (v % 2):128 * (v % 2) + 128]
+                    a = y * scale[v][i]
+                    s = shift[v][i]
+                    acc = a if acc is None else acc + a
+                    sub = s if sub is None else sub + s
+                vol[l, i] = av[0, i] * (acc - bv[0, i] * sub)
         return carry
 
-    lax.fori_loop(0, LEVELS, level, 0)
+    lax.fori_loop(0, LEVELS // LB, level, 0)
 
     for role, rows, target, kind in kinds:
         there = side_there if kind else col >= 0
@@ -396,7 +436,7 @@
     def _():
         side_dst[...] = jnp.zeros(side_dst.shape, f32)
 
-    up[...] = upsampled_tile(cb, *coarse_shape)
+    up[...] = upsampled_tile(cb, row_mat, col_mat, *coarse_shape)
 
     def pick(i, carry):
         rows = pl.ds(pl.multiple_of(8 * i, 8), 8)
@@ -497,7 +537,7 @@
 
 def on_device(reference_image, source_images, hypotheses, source_ids, coarse_disp, coarse_conf):
     shape = (coarse_disp.shape[0] * lax.axis_size("col"), coarse_disp.shape[1])
-    anywhere = pl.BlockSpec(memory_space=pl.ANY)
+    anywhere = pl.BlockSpec(memory_space=pltpu.HBM)
     n = SEG * 8
     return pl.pallas_call(
         functools.partial(stereo_kernel, shape),
@@ -529,11 +569,13 @@
             pltpu.VMEM((NM * 8, 256), f32),
             pltpu.VMEM((SRC + 1, NM, 8, 128), f32),
             pltpu.VMEM((SRC + 1, NM, 8, 128), f32),
-            pltpu.VMEM((2, n, 512), bf16),
-            pltpu.VMEM((n, 256), bf16),
-            pltpu.VMEM((2, n, 256), f32),
+            pltpu.VMEM((2, LB * n, 512), bf16),
+            pltpu.VMEM((LB * n, 256), bf16),
+            pltpu.VMEM((2, LB * n, 256), f32),
             pltpu.VMEM((LEVELS, SEG, 8, 128), f32),
             pltpu.VMEM((512, 128), f32),
+            pltpu.VMEM((ROWS, 32), bf16),
+            pltpu.VMEM((COLS, min(256, coarse_disp.shape[1])), bf16),
             pltpu.SemaphoreType.DMA((5,)),
             pltpu.SemaphoreType.DMA((1,)),
             pltpu.SemaphoreType.DMA((13,)),
@@ -541,7 +583,8 @@
             pltpu.SemaphoreType.DMA((16,)),
             pltpu.SemaphoreType.DMA((2,)),
         ],
-        compiler_params=pltpu.CompilerParams(collective_id=0, has_side_effects=True),
+        compiler_params=pltpu.CompilerParams(
+            collective_id=0, has_side_effects=True, vmem_limit_bytes=VMEM_LIMIT),
     )(source_ids, reference_image, source_images, hypotheses, coarse_disp, coarse_conf)
 
 

time: 42.4 us -> 35.3 us (0.83)
  the two profiles are of different devices: /device:TPU:9 before, /device:TPU:255 now
where the time goes in v4:
time: 35.3 us; the launch traced here: 35.2 us
  Pallas kernels  33.6 us (95%)
  local copies, waits for them, and re-layouts  1.57 us (4%)
    pallas_call x1, Pallas kernels, on_device(): pl.pallas_call(functools.partial(stereo_kernel, shape), out_shape=jax.Sha...  33.6 us
    unnamed x1, local copies, waits for them, and re-layouts  1.57 us

profile of v4, /device:TPU:255, one launch (start us, length us, event | category | flops | bytes accessed | tf_op | source)
XLA Modules:
  0.0 35.2 jit_solution(13994786315712874528)
XLA Ops:
  0.0 33.6 %shard_map.64 = f32[128,256]{1,0:T(8,128)} custom-call(s32[4]{0:T(128)} %ids.1, f32[128,256]{1,0:T(8,128)} %ref_in.1, f32[4,128,256]{2,1,0:T(8,128)} %src_in.1, s32[8,128,256]{2,1,0:T(8,128)} %hyp_in.1, f32[32,512]{1,0:T(8,128)} %disp_in.1, f32[32,512]{1,0:T(8,128)} %conf_in.1), custom_call_target="tpu_custom_call" | custom-call | tf_op jit(solution)/shard_map/pallas_call | solution.py:542
  33.6 1.6 %copy.8 = f32[128,256]{1,0:T(8,128)} copy(f32[128,256]{1,0:T(8,128)} %shard_map.64) | data formatting | bytes 262144

commit v5 on v4

--- a/solution.py
+++ b/solution.py
@@ -29,7 +29,7 @@
 NK = SEG + 2 * R
 NM = SEG + SHIFT
 HL = 2 * R
-LB = 2
+LB = 4
 VMEM_LIMIT = 60 * 1024 * 1024
 bf16 = jnp.bfloat16
 f32 = jnp.float32

time: 35.3 us -> 35.3 us (level)
  no operation moved by 1% of the time
where the time goes in v5:
time: 35.3 us; the launch traced here: 35.2 us
  Pallas kernels  33.6 us (95%)
  local copies, waits for them, and re-layouts  1.57 us (4%)
    pallas_call x1, Pallas kernels, on_device(): pl.pallas_call(functools.partial(stereo_kernel, shape), out_shape=jax.Sha...  33.6 us
    unnamed x1, local copies, waits for them, and re-layouts  1.57 us

profile of v5, /device:TPU:255, one launch (start us, length us, event | category | flops | bytes accessed | tf_op | source)
XLA Modules:
  0.0 35.2 jit_solution(8190126694965287512)
XLA Ops:
  0.0 33.6 %shard_map.64 = f32[128,256]{1,0:T(8,128)} custom-call(s32[4]{0:T(128)} %ids.1, f32[128,256]{1,0:T(8,128)} %ref_in.1, f32[4,128,256]{2,1,0:T(8,128)} %src_in.1, s32[8,128,256]{2,1,0:T(8,128)} %hyp_in.1, f32[32,512]{1,0:T(8,128)} %disp_in.1, f32[32,512]{1,0:T(8,128)} %conf_in.1), custom_call_target="tpu_custom_call" | custom-call | tf_op jit(solution)/shard_map/pallas_call | solution.py:542
  33.6 1.6 %copy.8 = f32[128,256]{1,0:T(8,128)} copy(f32[128,256]{1,0:T(8,128)} %shard_map.64) | data formatting | bytes 262144
